TPU v7x, 32 devices: a whole 2x2x4 slice. The times are simulated.
32 devices in a mesh: dp: 8 (over y, x, core), pencil: 4 (over z).
Axes of the slice: x: 2, y: 2, z: 4, core: 2. Of those that a mesh axis runs over, the one named last changes fastest.
Arguments:
- field: bfloat16 [8, 64, 64, 64, 128], P('dp', 'pencil'), may hold values from -6 to 6
- cotangent: bfloat16 [8, 64, 64, 64, 128], P('dp', 'pencil'), may hold values from -6 to 6
- w_spec: bfloat16 [16, 16, 16, 64, 128], P('dp', 'pencil'), may hold values from -6 to 6
- w_local: bfloat16 [64, 64], replicated, may hold values from -0.75 to 0.75
Outputs:
- grad_field: bfloat16 [8, 64, 64, 64, 128], P('dp', 'pencil')
- grad_w: float32 [16, 16, 16, 64, 128], P('dp', 'pencil')
All inputs are finite; a program needn't handle non-finite values.
Results may differ from a plain program's by a relative error of at most 0.02.
Values may be sent and summed in bfloat16 or wider, within the bound.
No kernel may reach another device: no remote copies, remote signals or barrier semaphores. Data moves between devices by JAX's collectives and lax.ppermute only.
A program may use at most 192 MiB of HBM per device.

v0:
```python
import math

import jax
import jax.numpy as jnp
from jax import lax
from jax.sharding import PartitionSpec as P

NX = 64
NY = 64
NZ = 128
CH = 64
MX = 16
MY = 16
MZ = 16


HIGHEST = lax.Precision.HIGHEST


def phase_pair(length, mode_count, signed):
    position = jnp.arange(length, dtype=jnp.int32)
    indices = jnp.arange(mode_count, dtype=jnp.int32)
    frequency = (
        jnp.where(indices < mode_count // 2, indices, indices - mode_count) if signed else indices
    )
    product = jnp.mod(position[:, None] * frequency[None, :], length).astype(jnp.float32)
    angles = product * (2.0 * math.pi / length)
    return (jnp.cos(angles), jnp.sin(angles))


def grid_tables():
    cos_x, sin_x = phase_pair(NX, MX, True)
    cos_y, sin_y = phase_pair(NY, MY, True)
    cos_z, sin_z = phase_pair(NZ, MZ, False)
    forward_z = jnp.concatenate([cos_z, -sin_z], 1).astype(jnp.bfloat16)
    weight_z = jnp.where(jnp.arange(MZ, dtype=jnp.int32) == 0, 1.0, 2.0).astype(jnp.float32) / (
        NX * NY * NZ
    )
    inverse_z = jnp.concatenate([cos_z * weight_z, -sin_z * weight_z], 1).T
    adjoint_z = jnp.concatenate([cos_z, -sin_z], 1).T
    spectrum_scale = jnp.concatenate([weight_z, weight_z])
    return (cos_x, sin_x, cos_y, sin_y, forward_z, inverse_z, adjoint_z, spectrum_scale)


def rotate_half(values):
    middle = values.shape[-1] // 2
    return jnp.concatenate([values[..., middle:], -values[..., :middle]], -1)


def along_y(values, cosines, sine_table, inverse):
    pattern = "xjck,yj->xyck" if inverse else "xyck,yj->xjck"
    factor = -1.0 if inverse else 1.0
    direct = jnp.einsum(pattern, values, cosines, precision=HIGHEST)
    turned = jnp.einsum(pattern, rotate_half(values), sine_table, precision=HIGHEST)
    return direct + factor * turned


def along_x(values, cosines, sine_table, inverse):
    pattern = "jbck,xj->xbck" if inverse else "xbck,xj->jbck"
    factor = -1.0 if inverse else 1.0
    direct = jnp.einsum(pattern, values, cosines, precision=HIGHEST)
    turned = jnp.einsum(pattern, rotate_half(values), sine_table, precision=HIGHEST)
    return direct + factor * turned


def z_forward(field_in, matrix):
    shape_in = field_in.shape
    product = jnp.dot(
        field_in.reshape(-1, shape_in[-1]), matrix, preferred_element_type=jnp.float32
    )
    return product.reshape(shape_in[:-1] + (matrix.shape[1],))


def z_back(values, matrix):
    shape_in = values.shape
    product = jnp.dot(
        values.reshape(-1, shape_in[-1]),
        matrix,
        precision=HIGHEST,
        preferred_element_type=jnp.float32,
    )
    return product.reshape(shape_in[:-1] + (matrix.shape[1],))


def gelu_slope(pre):
    normal_cdf = 0.5 * (1.0 + lax.erf(pre * (1.0 / math.sqrt(2.0))))
    return normal_cdf + pre * jnp.exp(-0.5 * pre * pre) * (1.0 / math.sqrt(2.0 * math.pi))


def apply_modes(coeffs, weights):
    real_part = coeffs[..., :MZ]
    imag_part = coeffs[..., MZ:]
    from_real = jnp.einsum(
        "sabik,abkio->sabok", real_part, weights, preferred_element_type=jnp.float32
    )
    from_imag = jnp.einsum(
        "sabik,abkio->sabok", imag_part, weights, preferred_element_type=jnp.float32
    )
    out_real = from_real[:, :, :, :CH] - from_imag[:, :, :, CH:]
    out_imag = from_real[:, :, :, CH:] + from_imag[:, :, :, :CH]
    return jnp.concatenate([out_real, out_imag], -1)


def paired(g_modes):
    g_real = g_modes[..., :MZ]
    g_imag = g_modes[..., MZ:]
    return (jnp.concatenate([g_real, g_imag], -2), jnp.concatenate([g_imag, -g_real], -2))


def adjoint_modes(g_modes, weights):
    paired_one, paired_two = paired(g_modes)
    back_real = jnp.einsum(
        "abkio,sabok->sabik", weights, paired_one, preferred_element_type=jnp.float32
    )
    back_imag = jnp.einsum(
        "abkio,sabok->sabik", weights, paired_two, preferred_element_type=jnp.float32
    )
    return jnp.concatenate([back_real, back_imag], -1)


def mode_grads(u_modes, g_modes):
    paired_one, paired_two = paired(g_modes)
    from_real = jnp.einsum(
        "sabik,sabok->abkio", u_modes[..., :MZ], paired_one, preferred_element_type=jnp.float32
    )
    from_imag = jnp.einsum(
        "sabik,sabok->abkio", u_modes[..., MZ:], paired_two, preferred_element_type=jnp.float32
    )
    return from_real + from_imag


def to_modes(field_in, tables):
    cos_x, sin_x, cos_y, sin_y, forward_z = (tables[0], tables[1], tables[2], tables[3], tables[4])
    sectioned = along_y(z_forward(field_in, forward_z), cos_y, sin_y, False)
    arrived = lax.all_to_all(
        sectioned.astype(jnp.bfloat16), "pencil", split_axis=1, concat_axis=0, tiled=True
    ).astype(sectioned.dtype)
    return along_x(arrived, cos_x, sin_x, False)


def to_grid(coeffs, tables, matrix):
    cos_x, sin_x, cos_y, sin_y = (tables[0], tables[1], tables[2], tables[3])
    sectioned = along_x(coeffs, cos_x, sin_x, True)
    arrived = lax.all_to_all(
        sectioned.astype(jnp.bfloat16), "pencil", split_axis=0, concat_axis=1, tiled=True
    ).astype(sectioned.dtype)
    return z_back(along_y(arrived, cos_y, sin_y, True), matrix)


def to_owner(coeffs):
    return lax.all_to_all(coeffs[None], "dp", split_axis=1, concat_axis=0, tiled=True)


def from_owner(coeffs):
    return lax.all_to_all(
        coeffs.astype(jnp.bfloat16), "dp", split_axis=0, concat_axis=1, tiled=True
    ).astype(coeffs.dtype)[0]


def body(field, cotangent, w_spec, w_local):
    tables = grid_tables()
    inverse_z, adjoint_z, spectrum_scale = (tables[5], tables[6], tables[7])
    sample = field[0]
    target = cotangent[0]
    u_modes = to_modes(sample, tables).astype(jnp.bfloat16)
    u_sent = to_owner(u_modes)
    v_modes = from_owner(apply_modes(u_sent, w_spec))
    values = to_grid(v_modes, tables, inverse_z)
    bypass = jnp.einsum("xycz,co->xyoz", sample, w_local, preferred_element_type=jnp.float32)
    slope_in = (target.astype(jnp.float32) * gelu_slope(values + bypass)).astype(jnp.bfloat16)
    g_modes = (to_modes(slope_in, tables) * spectrum_scale).astype(jnp.bfloat16)
    g_sent = to_owner(g_modes)
    grad_w = mode_grads(u_sent, g_sent)
    back_modes = from_owner(adjoint_modes(g_sent, w_spec))
    spread = jnp.einsum("xyoz,co->xycz", slope_in, w_local, preferred_element_type=jnp.float32)
    grad_sample = (to_grid(back_modes, tables, adjoint_z) + spread).astype(jnp.bfloat16)
    return (grad_sample[None], grad_w)


def solution(mesh):
    placed = (
        P("dp", "pencil", None, None, None),
        P("dp", "pencil", None, None, None),
        P("dp", "pencil", None, None, None),
        P(),
    )
    return jax.shard_map(
        body,
        mesh=mesh,
        in_specs=placed,
        out_specs=(P("dp", "pencil", None, None, None), P("dp", "pencil", None, None, None)),
        check_vma=False,
    )
```

profile of v0, /device:TPU:1, one launch (start us, length us, event | category | flops | bytes accessed | tf_op | source)
XLA Modules:
  0.0 624.4 jit_solution(11396002649751547669)
XLA Ops:
  0.7 15.0 %convolution_bitcast_fusion = f32[65536,32]{0,1:T(8,128)} fusion(bf16[65536,128]{1,0:T(8,128)(2,1)} %bitcast.173, f32[128,16]{0,1:T(8,128)S(1)} %get-tuple-element.28, f32[128,16]{0,1:T(8,128)S(1)} %get-tuple-element.29), kind=kOutput, calls=%fused_computation | convolution fusion | flops 536887296 | bytes 25182208 | tf_op jit(solution)/shard_map/dot_general | solution.py:68
  15.7 12.7 %reshape.60 = f32[16,64,64,32]{2,1,0,3:T(8,128)} reshape(f32[65536,32]{0,1:T(8,128)} %convolution_bitcast_fusion) | data formatting | bytes 16777216 | tf_op jit(solution)/shard_map/reshape | solution.py:71
  28.4 13.6 %fusion.227 = (f32[16,64,64,16]{2,1,3,0:T(8,128)}, f32[16,64,64,16]{2,1,3,0:T(8,128)}) fusion(f32[16,64,64,32]{2,1,0,3:T(8,128)} %reshape.60), kind=kLoop, calls=%fused_computation.242 | loop fusion | flops 1048576 | bytes 16777216 | tf_op jit(solution)/shard_map/slice | solution.py:47
  42.0 14.0 %fusion.8 = f32[16,16,64,32]{2,0,3,1:T(8,128)} fusion(f32[16,64,64,16]{2,1,3,0:T(8,128)} %get-tuple-element.5, f32[16,64,64,16]{2,1,3,0:T(8,128)} %get-tuple-element.4, s32[16]{0:T(128)S(1)} %compare_select_fusion), kind=kOutput, calls=%fused_computation.12 | convolution fusion | flops 404764672 | bytes 10485824 | tf_op jit(solution)/shard_map/xyck,yj->xjck/dot_general | solution.py:54
  56.0 10.0 %fusion.45 = bf16[16,16,64,32]{2,1,3,0:T(8,128)(2,1)S(1)} fusion(f32[16,16,64,32]{2,0,3,1:T(8,128)} %fusion.8, s32[16]{0:T(128)S(1)} %compare_select_fusion, f32[16,64,64,32]{2,1,0,3:T(8,128)S(1)} %bitcast.172), kind=kOutput, calls=%fused_computation.61 | convolution fusion | flops 403716096 | bytes 11534400 | tf_op jit(solution)/shard_map/xyck,yj->xjck/dot_general | solution.py:53
  71.3 30.2 %all_to_all.114 = bf16[4,2,65536]{2,1,0:T(2,128)(2,1)} all-to-all(bf16[4,2,65536]{2,1,0:T(2,128)(2,1)S(1)} %reshape.69), channel_id=1, replica_groups=mesh['dp'=8,'pencil'=4] {'pencil'}, dimensions={0} | all-to-all | bytes 2097152 | tf_op jit(solution)/shard_map/all_to_all | solution.py:135
  113.4 11.0 %all_to_all.115 = bf16[8,2,8192]{2,1,0:T(2,128)(2,1)S(1)} all-to-all(bf16[8,2,8192]{2,1,0:T(2,128)(2,1)S(1)} %reshape.71), channel_id=1, replica_groups=mesh['dp'=8,'pencil'=4] {'dp'}, dimensions={0} | all-to-all | bytes 524288 | tf_op jit(solution)/shard_map/all_to_all | solution.py:151
  154.5 25.2 %all-to-all-done.3 = bf16[4,2,65536]{2,1,0:T(2,128)(2,1)S(1)} async-done(((bf16[4,2,65536]{2,1,0:T(2,128)(2,1)}), bf16[4,2,65536]{2,1,0:T(2,128)(2,1)S(1)}, u32[]{:S(2)}, u32[]{:S(2)}) %all-to-all-start.3) | async-done | bytes 1048608 | tf_op jit(solution)/shard_map/all_to_all | solution.py:144
  184.2 10.6 %fusion.43 = f32[64,16,64,32]{2,0,3,1:T(8,128)} fusion(bf16[16,16,64,32]{2,3,1,0:T(8,128)(2,1)S(1)} %bitcast.176, s32[16]{0:T(128)S(1)} %compare_select_fusion), kind=kOutput, calls=%fused_computation.59 | convolution fusion | flops 402667520 | bytes 9437248 | tf_op jit(solution)/shard_map/xjck,yj->xyck/dot_general | solution.py:53
  195.9 19.0 %add_bitcast_fusion.1 = f32[16,64,64,32]{2,1,3,0:T(8,128)} fusion(f32[64,16,64,32]{2,0,3,1:T(8,128)} %fusion.43, f32[16,16,64,16]{2,1,3,0:T(8,128)S(1)} %get-tuple-element.11, f32[16,16,64,16]{2,1,3,0:T(8,128)S(1)} %get-tuple-element.10, s32[16]{0:T(128)S(1)} %compare_select_fusion), kind=kOutput, calls=%fused_computation.28 | convolution fusion | flops 407386112 | bytes 18874432 | tf_op jit(solution)/shard_map/xjck,yj->xyck/dot_general | solution.py:54
  214.9 65.2 %fusion.20 = f32[16,64,64,128]{3,2,1,0:T(8,128)} fusion(f32[16,64,64,32]{2,1,3,0:T(8,128)} %add_bitcast_fusion.1, f32[128,16]{0,1:T(8,128)S(1)} %get-tuple-element.27, f32[128,16]{0,1:T(8,128)S(1)} %get-tuple-element.26), kind=kOutput, calls=%fused_computation.25 | convolution fusion | flops 3221229568 | bytes 41959424 | tf_op jit(solution)/shard_map/dot_general | solution.py:76
  280.2 31.4 %fusion.5 = bf16[16,64,64,128]{3,2,1,0:T(8,128)(2,1)} fusion(f32[16,64,64,128]{3,2,1,0:T(8,128)} %fusion.20, bf16[1,16,64,64,128]{4,3,2,1,0:T(8,128)(2,1)} %param.5, bf16[1,16,64,64,128]{4,3,2,1,0:T(8,128)(2,1)} %param.4, bf16[64,64]{1,0:T(8,128)(2,1)S(1)} %copy-done.7), kind=kOutput, calls=%fused_computation.7 | convolution fusion | flops 1174405120 | bytes 83894272 | tf_op jit(solution)/shard_map/xycz,co->xyoz/dot_general | solution.py:169
  311.6 19.4 %fusion.98 = f32[16,64,64,32]{2,3,1,0:T(8,128)S(1)} fusion(bf16[16,64,64,128]{3,2,1,0:T(8,128)(2,1)} %fusion.5, f32[128,16]{0,1:T(8,128)S(1)} %get-tuple-element.28, f32[128,16]{0,1:T(8,128)S(1)} %get-tuple-element.29), kind=kOutput, calls=%fused_computation.122 | convolution fusion | flops 536887296 | bytes 25182208 | tf_op jit(solution)/shard_map/dot_general | solution.py:68
  337.7 12.0 %pad_maximum_fusion = f32[16,64,64,32]{2,3,1,0:T(8,128)} fusion(f32[16,64,64,16]{2,3,1,0:T(8,128)} %get-tuple-element.3, f32[16,64,64,16]{2,3,1,0:T(8,128)} %get-tuple-element.2), kind=kLoop, calls=%fused_computation.16 | loop fusion | flops 2097152 | bytes 16777216 | tf_op jit(solution)/shard_map/concatenate | solution.py:47
  349.8 23.7 %fusion.16 = f32[16,16,64,32]{2,0,3,1:T(8,128)} fusion(f32[16,64,64,32]{2,3,1,0:T(8,128)} %pad_maximum_fusion, s32[16]{0:T(128)S(1)} %compare_select_fusion), kind=kOutput, calls=%fused_computation.21 | convolution fusion | flops 402667520 | bytes 10485824 | tf_op jit(solution)/shard_map/xyck,yj->xjck/dot_general | solution.py:54
  373.5 17.0 %fusion.38 = bf16[16,16,64,32]{2,1,3,0:T(8,128)(2,1)S(1)} fusion(f32[16,16,64,32]{2,0,3,1:T(8,128)} %fusion.16, f32[16,64,64,32]{2,3,1,0:T(8,128)S(1)} %fusion.98, s32[16]{0:T(128)S(1)} %compare_select_fusion), kind=kOutput, calls=%fused_computation.50 | convolution fusion | flops 403716096 | bytes 11534400 | tf_op jit(solution)/shard_map/xyck,yj->xjck/dot_general | solution.py:53
  400.5 25.2 %all-to-all-done.4 = bf16[4,2,65536]{2,1,0:T(2,128)(2,1)S(1)} async-done(((bf16[4,2,65536]{2,1,0:T(2,128)(2,1)}), bf16[4,2,65536]{2,1,0:T(2,128)(2,1)S(1)}, u32[]{:S(2)}, u32[]{:S(2)}) %all-to-all-start.4) | async-done | bytes 1048608 | tf_op jit(solution)/shard_map/all_to_all | solution.py:135
  435.9 9.5 %all_to_all.117 = bf16[8,2,8192]{2,1,0:T(2,128)(2,1)S(1)} all-to-all(bf16[8,2,8192]{2,1,0:T(2,128)(2,1)S(1)} %reshape.79), channel_id=1, replica_groups=mesh['dp'=8,'pencil'=4] {'dp'}, dimensions={0} | all-to-all | bytes 524288 | tf_op jit(solution)/shard_map/all_to_all | solution.py:151
  449.4 9.3 %all_to_all.118 = bf16[8,2,8192]{2,1,0:T(2,128)(2,1)S(1)} all-to-all(bf16[8,2,8192]{2,1,0:T(2,128)(2,1)S(1)} %reshape.81), channel_id=1, replica_groups=mesh['dp'=8,'pencil'=4] {'dp'}, dimensions={0} | all-to-all | bytes 524288 | tf_op jit(solution)/shard_map/all_to_all | solution.py:155
  481.5 20.3 %all-to-all-done.7 = bf16[4,2,65536]{2,1,0:T(2,128)(2,1)S(1)} async-done(((bf16[4,2,65536]{2,1,0:T(2,128)(2,1)}), bf16[4,2,65536]{2,1,0:T(2,128)(2,1)S(1)}, u32[]{:S(2)}, u32[]{:S(2)}) %all-to-all-start.7) | async-done | bytes 1048608 | tf_op jit(solution)/shard_map/all_to_all | solution.py:144
  506.4 10.6 %fusion.41 = f32[64,16,64,32]{2,0,3,1:T(8,128)} fusion(bf16[16,16,64,32]{2,3,1,0:T(8,128)(2,1)S(1)} %bitcast.178, s32[16]{0:T(128)S(1)} %compare_select_fusion), kind=kOutput, calls=%fused_computation.56 | convolution fusion | flops 402667520 | bytes 9437248 | tf_op jit(solution)/shard_map/xjck,yj->xyck/dot_general | solution.py:53
  518.1 19.0 %add_bitcast_fusion = f32[16,64,64,32]{2,1,3,0:T(8,128)} fusion(f32[64,16,64,32]{2,0,3,1:T(8,128)} %fusion.41, f32[16,16,64,16]{2,1,3,0:T(8,128)S(1)} %get-tuple-element.7, f32[16,16,64,16]{2,1,3,0:T(8,128)S(1)} %get-tuple-element.6, s32[16]{0:T(128)S(1)} %compare_select_fusion), kind=kOutput, calls=%fused_computation.27 | convolution fusion | flops 407386112 | bytes 18874432 | tf_op jit(solution)/shard_map/xjck,yj->xyck/dot_general | solution.py:54
  537.1 64.8 %fusion.14 = f32[16,64,64,128]{3,2,1,0:T(8,128)} fusion(f32[16,64,64,32]{2,1,3,0:T(8,128)} %add_bitcast_fusion, f32[128,16]{0,1:T(8,128)S(1)} %get-tuple-element.28, f32[128,16]{0,1:T(8,128)S(1)} %get-tuple-element.29), kind=kOutput, calls=%fused_computation.19 | convolution fusion | flops 3221229568 | bytes 41959424 | tf_op jit(solution)/shard_map/dot_general | solution.py:76
  602.0 22.2 %fusion.7 = bf16[1,16,64,64,128]{4,3,2,1,0:T(8,128)(2,1)} fusion(f32[16,64,64,128]{3,2,1,0:T(8,128)} %fusion.14, bf16[16,64,64,128]{3,2,1,0:T(8,128)(2,1)} %fusion.5, bf16[64,64]{1,0:T(8,128)(2,1)S(1)} %copy-done.7), kind=kOutput, calls=%fused_computation.11 | convolution fusion | flops 1090519040 | bytes 67117056 | tf_op jit(solution)/shard_map/xyoz,co->xycz/dot_general | solution.py:175
  (96 shorter events, 112.2 us)
Async XLA Ops:
  0.6 124.2 %copy-start = (bf16[2,4,16,64,128]{4,3,2,1,0:T(8,128)(2,1)S(1)}, bf16[2,4,16,64,128]{4,3,2,1,0:T(8,128)(2,1)}, u32[]{:S(2)}) copy-start(bf16[2,4,16,64,128]{4,3,2,1,0:T(8,128)(2,1)} %param.6) | copy-start | bytes 6291460
  28.4 27.6 %slice-start = ((s8[16777216]{0:T(1024)(128)(4,1)}), s8[4194304]{0:T(1024)(128)(4,1)S(1)}, s32[]{:S(2)}) async-start(s8[16777216]{0:T(1024)(128)(4,1)} %bitcast.171), calls=%async_computation.8 | async-start | bytes 8388608
  28.4 27.6 %slice-start.1 = ((s8[16777216]{0:T(1024)(128)(4,1)}), s8[4194304]{0:T(1024)(128)(4,1)S(1)}, s32[]{:S(2)}) async-start(s8[16777216]{0:T(1024)(128)(4,1)} %bitcast.171), calls=%async_computation.9 | async-start | bytes 8388608
  28.4 27.6 %slice-start.2 = ((s8[16777216]{0:T(1024)(128)(4,1)}), s8[4194304]{0:T(1024)(128)(4,1)S(1)}, s32[]{:S(2)}) async-start(s8[16777216]{0:T(1024)(128)(4,1)} %bitcast.171), calls=%async_computation.10 | async-start | bytes 8388608
  42.0 14.0 %slice-start.3 = ((s8[16777216]{0:T(1024)(128)(4,1)}), s8[4194304]{0:T(1024)(128)(4,1)S(1)}, s32[]{:S(2)}) async-start(s8[16777216]{0:T(1024)(128)(4,1)} %bitcast.171), calls=%async_computation.11 | async-start | bytes 8388608
  124.8 0.7 copy-start.4
  124.8 0.8 copy-start.6
  150.5 29.2 %all-to-all-start.3 = ((bf16[4,2,65536]{2,1,0:T(2,128)(2,1)}), bf16[4,2,65536]{2,1,0:T(2,128)(2,1)S(1)}, u32[]{:S(2)}, u32[]{:S(2)}) async-start(bf16[4,2,65536]{2,1,0:T(2,128)(2,1)} %reshape.75), calls=%async_computation.3 | async-start | bytes 2097152 | tf_op jit(solution)/shard_map/all_to_all | solution.py:144
  214.9 65.2 %copy-start.7 = (bf16[64,64]{1,0:T(8,128)(2,1)S(1)}, bf16[64,64]{1,0:T(8,128)(2,1)}, u32[]{:S(2)}) copy-start(bf16[64,64]{1,0:T(8,128)(2,1)} %param.7) | copy-start | bytes 24580
  396.6 29.0 %all-to-all-start.4 = ((bf16[4,2,65536]{2,1,0:T(2,128)(2,1)}), bf16[4,2,65536]{2,1,0:T(2,128)(2,1)S(1)}, u32[]{:S(2)}, u32[]{:S(2)}) async-start(bf16[4,2,65536]{2,1,0:T(2,128)(2,1)} %reshape.77), calls=%async_computation.4 | async-start | bytes 2097152 | tf_op jit(solution)/shard_map/all_to_all | solution.py:135
  446.0 2.9 copy-start.1
  446.0 2.9 copy-start.3
  472.6 29.2 %all-to-all-start.7 = ((bf16[4,2,65536]{2,1,0:T(2,128)(2,1)}), bf16[4,2,65536]{2,1,0:T(2,128)(2,1)S(1)}, u32[]{:S(2)}, u32[]{:S(2)}) async-start(bf16[4,2,65536]{2,1,0:T(2,128)(2,1)} %reshape.83), calls=%async_computation.7 | async-start | bytes 2097152 | tf_op jit(solution)/shard_map/all_to_all | solution.py:144
  476.6 2.0 copy-start.2
  476.6 2.0 copy-start.5
where the time goes:
time: 630 us; the launch traced here: 624 us
  matrix products  370 us (59%)
  waiting for transfers between devices  70.6 us (11%)
  blocking collectives  69.3 us (11%)
  local copies, waits for them, and re-layouts  63 us (10%)
  other arithmetic  38.9 us (6%)
  starting transfers between devices  11.6 us (2%)
    dot_general x2, matrix products, z_back(): jnp.dot(values.reshape(-1, shape_in[-1]), matrix, precision=HIGHEST, pref...  130 us
    dot_general x4, matrix products, along_y(): jnp.einsum(pattern, rotate_half(values), sine_table, precision=HIGHEST)  75.8 us
    dot_general x4, matrix products, along_y(): direct = jnp.einsum(pattern, values, cosines, precision=HIGHEST)  48.2 us
    all_to_all x2, waiting for transfers between devices, to_grid(): lax.all_to_all(sectioned.astype(jnp.bfloat16), 'pencil', split_axis=0, co...  45.4 us
    dot_general x2, matrix products, z_forward(): jnp.dot(field_in.reshape(-1, shape_in[-1]), matrix, preferred_element_typ...  34.4 us
    unnamed x41, local copies, waits for them, and re-layouts  32 us
    dot_general x1, matrix products, body(): jnp.einsum('xycz,co->xyoz', sample, w_local, preferred_element_type=jnp.f...  31.4 us
    all_to_all x1, blocking collectives, to_modes(): lax.all_to_all(sectioned.astype(jnp.bfloat16), 'pencil', split_axis=1, co...  30.2 us
  transfers between devices with their start and end apart: 3, of which 3 were waited for; matrix products, arithmetic and copies ran while one was open for 1% of the time, Pallas kernels for 0%

commit v1 on v0

v1 whole, which is shorter than its diff:
```python
import functools
import math

import jax
import jax.numpy as jnp
import numpy as np
from jax import lax
from jax.experimental import pallas as pl
from jax.experimental.pallas import tpu as pltpu
from jax.sharding import PartitionSpec as P

F32 = jnp.float32
BF16 = jnp.bfloat16
SUB = 16
LIMIT = 60 * 1024 * 1024


def phases(length, count, signed):
    position = np.arange(length)
    index = np.arange(count)
    freq = np.where(index < count // 2, index, index - count) if signed else index
    angle = np.mod(position[:, None] * freq[None, :], length) * (2.0 * math.pi / length)
    return np.cos(angle), np.sin(angle)


def kron_tables(nx, mx, parts):
    cos_x, sin_x = phases(nx, mx, True)
    eye = np.eye(SUB)
    local = nx // parts
    fwd, inv = [], []
    for p in range(parts):
        c = cos_x[p * local : (p + 1) * local]
        s = sin_x[p * local : (p + 1) * local]
        fwd.append(np.concatenate([np.kron(c.T, eye), np.kron(s.T, eye)], 1))
        inv.append(np.concatenate([np.kron(c, eye), np.kron(s, eye)], 1))
    return np.stack(fwd).astype(jnp.bfloat16), np.stack(inv).astype(jnp.bfloat16)


def grid_tables(ny, my, nz, mz):
    cos_y, sin_y = phases(ny, my, True)
    cos_z, sin_z = phases(nz, mz, False)
    cos_z = cos_z.astype(jnp.bfloat16).astype(np.float32)
    sin_z = sin_z.astype(jnp.bfloat16).astype(np.float32)
    ytab = np.stack([np.repeat(cos_y, mz, 1), np.repeat(sin_y, mz, 1)]).astype(np.float32)
    ztab = np.stack([np.tile(cos_z, (1, my)), np.tile(sin_z, (1, my))]).astype(np.float32)
    return ytab, ztab


def fill_basis(basis, ytab, ztab, yb, nz):
    cz = ztab[0]
    sz = ztab[1]
    for y in range(yb):
        cy = ytab[0, y : y + 1, :]
        sy = ytab[1, y : y + 1, :]
        re = cy * cz - sy * sz
        im = -(sy * cz + cy * sz)
        basis[y * nz : (y + 1) * nz, :] = jnp.concatenate([re, im], 1).astype(BF16)


def x_forward_store(acc, xf, out, mx, modes):
    xl, ch, _ = acc.shape
    groups = ch // SUB
    parts = []
    for g in range(groups):
        a = acc[:, g * SUB : (g + 1) * SUB, :].reshape(xl * SUB, 2 * modes).astype(BF16)
        re = a[:, :modes]
        im = a[:, modes:]
        rhs = jnp.concatenate(
            [jnp.concatenate([re, im], 1), jnp.concatenate([im, -re], 1)], 0
        )
        parts.append(jnp.dot(xf, rhs, preferred_element_type=F32))
    dp, pencil, jo, mo, _ = out.shape
    for j in range(mx):
        rows = slice(j * SUB, (j + 1) * SUB)
        block = jnp.concatenate(
            [part[rows, :modes] for part in parts] + [part[rows, modes:] for part in parts], 0
        )
        turned = block.T.astype(BF16)
        for q in range(pencil):
            out[j // jo, q, j % jo] = turned[q * mo : (q + 1) * mo, :]


def x_inverse_load(spec, turned, xi, half, xl, ch):
    pencil, dp, jo, mo, _ = spec.shape
    mx = dp * jo
    modes = pencil * mo
    for j in range(mx):
        block = jnp.concatenate([spec[q, j // jo, j % jo] for q in range(pencil)], 0)
        turned[j] = block.astype(F32).T.astype(BF16)
    for g in range(ch // SUB):
        re = turned[:, g * SUB : (g + 1) * SUB, :].reshape(mx * SUB, modes)
        im = turned[:, ch + g * SUB : ch + (g + 1) * SUB, :].reshape(mx * SUB, modes)
        rhs = jnp.concatenate(
            [jnp.concatenate([re, im], 1), jnp.concatenate([-im, re], 1)], 0
        )
        b = jnp.dot(xi, rhs, preferred_element_type=F32)
        half[:, g * SUB : (g + 1) * SUB, :] = b.reshape(xl, SUB, 2 * modes).astype(BF16)


def grid_rows(ref, x0, xn, yb):
    ch, nz = ref.shape[2], ref.shape[3]
    return jnp.concatenate(
        [ref[x0 : x0 + xn, y].reshape(xn * ch, nz) for y in range(yb)], 1
    )


def forward_kernel(rank, field, ytab, ztab, xf, out, basis, acc, *, xn):
    xl, yb, ch, nz = field.shape
    modes = ytab.shape[2]
    step = pl.program_id(0)

    @pl.when(step == 0)
    def _():
        acc[...] = jnp.zeros_like(acc)

    fill_basis(basis, ytab, ztab, yb, nz)
    for x0 in range(0, xl, xn):
        part = jnp.dot(grid_rows(field, x0, xn, yb), basis[...], preferred_element_type=F32)
        acc[x0 : x0 + xn] += part.reshape(xn, ch, 2 * modes)

    @pl.when(step == pl.num_programs(0) - 1)
    def _():
        x_forward_store(acc, xf[0], out, xf.shape[1] // SUB, modes)


def slope_kernel(
    rank, spec, field, cot, mix, ytab, ztab, xf, xi, slope, out, basis, acc, turned, half, *, xn
):
    xl, yb, ch, nz = field.shape
    modes = ytab.shape[2]
    step = pl.program_id(0)

    @pl.when(step == 0)
    def _():
        acc[...] = jnp.zeros_like(acc)
        x_inverse_load(spec, turned, xi[0], half, xl, ch)

    fill_basis(basis, ytab, ztab, yb, nz)
    for x0 in range(0, xl, xn):
        rows = half[x0 : x0 + xn].reshape(xn * ch, 2 * modes)
        pre = lax.dot_general(
            rows, basis[...], (((1,), (1,)), ((), ())), preferred_element_type=F32
        )
        pre = pre + jnp.dot(
            mix[...], grid_rows(field, x0, xn, yb), preferred_element_type=F32
        )
        q = pre * (1.0 / math.sqrt(2.0))
        bell = jnp.exp(-(q * q)) * q
        gain = (0.5 + 0.5 * lax.erf(q)) + bell * (1.0 / math.sqrt(math.pi))
        value = (grid_rows(cot, x0, xn, yb).astype(F32) * gain).astype(BF16)
        for y in range(yb):
            slope[x0 : x0 + xn, y] = value[:, y * nz : (y + 1) * nz].reshape(xn, ch, nz)
        part = jnp.dot(value, basis[...], preferred_element_type=F32)
        acc[x0 : x0 + xn] += part.reshape(xn, ch, 2 * modes)

    @pl.when(step == pl.num_programs(0) - 1)
    def _():
        x_forward_store(acc, xf[0], out, xf.shape[1] // SUB, modes)


def inverse_kernel(rank, spec, slope, mix, ytab, ztab, xi, grad, basis, turned, half, *, xn):
    xl, yb, ch, nz = slope.shape
    modes = ytab.shape[2]

    @pl.when(pl.program_id(0) == 0)
    def _():
        x_inverse_load(spec, turned, xi[0], half, xl, ch)

    fill_basis(basis, ytab, ztab, yb, nz)
    for x0 in range(0, xl, xn):
        rows = half[x0 : x0 + xn].reshape(xn * ch, 2 * modes)
        total = lax.dot_general(
            rows, basis[...], (((1,), (1,)), ((), ())), preferred_element_type=F32
        )
        total = total + jnp.dot(
            mix[...], grid_rows(slope, x0, xn, yb), preferred_element_type=F32
        )
        total = total.astype(BF16)
        for y in range(yb):
            grad[x0 : x0 + xn, y] = total[:, y * nz : (y + 1) * nz].reshape(xn, ch, nz)


def other_half(values):
    return pltpu.roll(values, values.shape[-1] // 2, 1)


def gather_partials(received, store, samples, pencil, scale):
    modes = received.shape[1]
    for s in range(samples):
        total = received[s * pencil].astype(F32)
        for p in range(1, pencil):
            total = total + received[s * pencil + p].astype(F32)
        store[s * modes : (s + 1) * modes, :] = (total * scale).astype(BF16).astype(F32)


def mode_scale(modes, lanes, mz, size):
    k = lax.broadcasted_iota(jnp.int32, (modes, lanes), 0) % mz
    return jnp.where(k == 0, 1.0 / size, 2.0 / size).astype(F32)


def apply_kernel(received, weights, uhat, out, store, result, *, samples, pencil, mz, size):
    modes, ch, wide = weights.shape
    gather_partials(received, store, samples, pencil, 1.0)
    uhat[...] = store[...]
    sign = jnp.where(
        lax.broadcasted_iota(jnp.int32, (samples, wide), 1) < ch, -1.0, 1.0
    ).astype(F32)

    def one(m):
        rows = pl.ds(m, samples, stride=modes)
        u = store[rows, :]
        lhs = jnp.concatenate([u, other_half(u)], 0)[:, :ch].astype(BF16)
        both = jnp.dot(lhs, weights[m], preferred_element_type=F32)
        result[rows, :] = both[:samples] + sign * other_half(both[samples:])

    for m in range(modes):
        one(m)
    scale = mode_scale(modes, wide, mz, size)
    for s in range(samples):
        out[s] = (result[s * modes : (s + 1) * modes, :] * scale).astype(BF16)


def adjoint_kernel(
    received, weights, uhat, out, grad, store, result, *, samples, pencil, mz, size, total
):
    block, ch, wide = weights.shape
    step = pl.program_id(0)

    @pl.when(step == 0)
    def _():
        gather_partials(received, store, samples, pencil, mode_scale(total, wide, mz, size))

    low = lax.broadcasted_iota(jnp.int32, (samples, wide), 1) < ch
    sign = jnp.where(low, 1.0, -1.0).astype(F32)
    for i in range(block):
        rows = pl.ds(step * block + i, samples, stride=total)
        u = uhat[rows, :]
        g = store[rows, :]
        uu = jnp.concatenate([u, other_half(u)], 0)[:, :ch].astype(BF16)
        gg = jnp.concatenate([g, sign * other_half(g)], 0).astype(BF16)
        w = weights[i]
        both = lax.dot_general(
            gg, jnp.concatenate([w, w], 0), (((1,), (1,)), ((), ())), preferred_element_type=F32
        )
        result[rows, :] = jnp.where(low, both[:samples], both[samples:])
        grad[i] = lax.dot_general(
            uu, gg, (((0,), (0,)), ((), ())), preferred_element_type=F32
        )

    @pl.when(step == pl.num_programs(0) - 1)
    def _():
        for s in range(samples):
            out[s] = result[s * total : (s + 1) * total, :].astype(BF16)


def params():
    return pltpu.CompilerParams(
        dimension_semantics=("arbitrary",), vmem_limit_bytes=LIMIT
    )


def whole(shape):
    return pl.BlockSpec(shape, lambda i, r: (0,) * len(shape))


def make_body(dp, pencil):
    def body(field, cotangent, w_spec, w_local):
        sample = field[0]
        target = cotangent[0]
        xl, ny, ch, nz = sample.shape
        jo, lo, mz, _, wide = w_spec.shape
        nx, mx, my = xl * pencil, jo * dp, lo * pencil
        modes = my * mz
        mo = lo * mz
        samples = dp
        owned = jo * mo
        size = nx * ny * nz
        xn = min(xl, 4)
        rank = lax.axis_index("pencil").astype(jnp.int32).reshape(1)

        xf, xi = kron_tables(nx, mx, pencil)
        ytab, ztab = grid_tables(ny, my, nz, mz)
        weights = w_spec.reshape(owned, ch, wide)
        mix_out = jnp.kron(jnp.eye(xn, dtype=BF16), w_local.T)
        mix_in = jnp.kron(jnp.eye(xn, dtype=BF16), w_local)

        def grid_spec(yb):
            return pl.BlockSpec((xl, yb, ch, nz), lambda i, r: (0, i, 0, 0))

        def y_spec(yb):
            return pl.BlockSpec((2, None, yb, modes), lambda i, r: (0, i, 0, 0))

        def y_table(yb):
            return ytab.reshape(2, ny // yb, yb, modes)

        z_spec = whole(ztab.shape)
        ranked = lambda t: pl.BlockSpec((1,) + t.shape[1:], lambda i, r: (r[0], 0, 0))
        packed = (dp, pencil, jo, mo, 2 * ch)
        unpacked = (pencil, dp, jo, mo, 2 * ch)

        def call(kernel, yb, ins, outs, shapes, scratch, name, args):
            return pl.pallas_call(
                functools.partial(kernel, xn=xn),
                grid_spec=pltpu.PrefetchScalarGridSpec(
                    num_scalar_prefetch=1,
                    grid=(ny // yb,),
                    in_specs=ins,
                    out_specs=outs,
                    scratch_shapes=scratch,
                ),
                out_shape=shapes,
                compiler_params=params(),
                name=name,
            )(rank, *args)

        def basis(yb):
            return pltpu.VMEM((yb * nz, 2 * modes), BF16)

        acc = pltpu.VMEM((xl, ch, 2 * modes), F32)
        turned = pltpu.VMEM((mx, 2 * ch, modes), BF16)
        half = pltpu.VMEM((xl, ch, 2 * modes), BF16)
        spectrum = jax.ShapeDtypeStruct(packed, BF16)
        grid_shape = jax.ShapeDtypeStruct(sample.shape, BF16)

        def to_owner(values):
            flat = values.reshape((dp * pencil, owned, 2 * ch))
            return lax.all_to_all(flat, ("dp", "pencil"), 0, 0, tiled=True)

        def from_owner(values):
            sent = jnp.broadcast_to(values[:, None], (dp, pencil, owned, 2 * ch))
            got = lax.all_to_all(
                sent.reshape(dp * pencil, owned, 2 * ch), ("dp", "pencil"), 0, 0, tiled=True
            )
            got = got.reshape(dp, pencil, jo, mo, 2 * ch)
            return got.transpose(1, 0, 2, 3, 4)

        yb = 8
        s1 = call(
            forward_kernel,
            yb,
            [grid_spec(yb), y_spec(yb), z_spec, ranked(xf)],
            whole(packed),
            spectrum,
            [basis(yb), acc],
            "field_modes",
            (sample, y_table(yb), ztab, xf),
        )
        u_got = to_owner(s1)
        rows = pltpu.VMEM((samples * owned, 2 * ch), F32)
        sizes = dict(samples=samples, pencil=pencil, mz=mz, size=size)
        uhat, v_own = pl.pallas_call(
            functools.partial(apply_kernel, **sizes),
            out_shape=(
                jax.ShapeDtypeStruct((samples * owned, 2 * ch), F32),
                jax.ShapeDtypeStruct((samples, owned, 2 * ch), BF16),
            ),
            scratch_shapes=[rows, rows],
            compiler_params=pltpu.CompilerParams(vmem_limit_bytes=LIMIT),
            name="apply_modes",
        )(u_got, weights)
        v = from_owner(v_own)
        yb = 4
        slope, s2 = call(
            slope_kernel,
            yb,
            [
                whole(unpacked),
                grid_spec(yb),
                grid_spec(yb),
                whole(mix_out.shape),
                y_spec(yb),
                z_spec,
                ranked(xf),
                ranked(xi),
            ],
            (grid_spec(yb), whole(packed)),
            (grid_shape, spectrum),
            [basis(yb), acc, turned, half],
            "slope_modes",
            (v, sample, target, mix_out, y_table(yb), ztab, xf, xi),
        )
        g_got = to_owner(s2)
        steps = 8 if owned % 8 == 0 else 1
        block = owned // steps
        fixed = lambda shape: pl.BlockSpec(shape, lambda i: (0,) * len(shape))
        moving = pl.BlockSpec((block, ch, wide), lambda i: (i, 0, 0))
        du_own, grad_w = pl.pallas_call(
            functools.partial(adjoint_kernel, total=owned, **sizes),
            grid=(steps,),
            in_specs=[fixed(g_got.shape), moving, fixed(uhat.shape)],
            out_specs=(fixed((samples, owned, 2 * ch)), moving),
            out_shape=(
                jax.ShapeDtypeStruct((samples, owned, 2 * ch), BF16),
                jax.ShapeDtypeStruct((owned, ch, wide), F32),
            ),
            scratch_shapes=[rows, rows],
            compiler_params=params(),
            name="adjoint_modes",
        )(g_got, weights, uhat)
        du = from_owner(du_own)
        grad = call(
            inverse_kernel,
            yb,
            [
                whole(unpacked),
                grid_spec(yb),
                whole(mix_in.shape),
                y_spec(yb),
                z_spec,
                ranked(xi),
            ],
            grid_spec(yb),
            grid_shape,
            [basis(yb), turned, half],
            "grad_field",
            (du, slope, mix_in, y_table(yb), ztab, xi),
        )
        return grad[None], grad_w.reshape(jo, lo, mz, ch, wide)

    return body


def solution(mesh):
    split = P("dp", "pencil", None, None, None)
    return jax.shard_map(
        make_body(mesh.shape["dp"], mesh.shape["pencil"]),
        mesh=mesh,
        in_specs=(split, split, split, P()),
        out_specs=(split, split),
        check_vma=False,
    )
```

time: 630 us -> 229 us (0.36)
  matrix products: 370 us -> 0 us
  Pallas kernels: 0 us -> 98.7 us
  local copies, waits for them, and re-layouts: 63 us -> 8.28 us
  other arithmetic: 38.9 us -> 0.27 us
  waiting for transfers between devices: 70.6 us -> 50.5 us
    dot_general x28 -> x0, matrix products: 370 us -> none  [the longest x2 130 us: z_back(): jnp.dot(values.reshape(-1, shape_in[-1]), matrix, precision=HIGHEST, pref...]
    pallas_call x0 -> x5, Pallas kernels: none -> 98.7 us  [the longest x3 85.4 us: call(): pl.pallas_call(functools.partial(kernel, xn=xn), grid_spec=pltpu.Prefetch...]
    unnamed x41 -> x2, local copies, waits for them, and re-layouts: 32 us -> 0.01 us
    slice x8 -> x0, other arithmetic: 22.5 us -> none  [rotate_half(): return jnp.concatenate([values[..., middle:], -values[..., :middle]], -1)]
    all_to_all x3 -> x2, waiting for transfers between devices: 70.6 us -> 50.5 us  [from_owner(): lax.all_to_all(sent.reshape(dp * pencil, owned, 2 * ch), ('dp', 'pencil')...]
    concatenate x4 -> x0, other arithmetic: 12.3 us -> none  [the longest x1 12 us: rotate_half(): return jnp.concatenate([values[..., middle:], -values[..., :middle]], -1)]
    reshape x1 -> x2, local copies, waits for them, and re-layouts: 12.7 us -> 2.1 us  [from_owner(): got = got.reshape(dp, pencil, jo, mo, 2 * ch)]
    convert_element_type x4 -> x0, local copies, waits for them, and re-layouts: 9.07 us -> none  [the longest x2 5.34 us: to_grid(): sectioned.astype(jnp.bfloat16)]
  transfers between devices with their start and end apart: 3 -> 2, of which waited for: 3 -> 2; matrix products, arithmetic and copies ran while one was open for 1% -> 1% of each run, Pallas kernels for 0% -> 0%
where the time goes in v1:
time: 229 us; the launch traced here: 228 us
  Pallas kernels  98.7 us (43%)
  blocking collectives  63.1 us (28%)
  waiting for transfers between devices  50.5 us (22%)
  local copies, waits for them, and re-layouts  8.28 us (4%)
  starting transfers between devices  6.3 us (3%)
    pallas_call x3, Pallas kernels, call(): pl.pallas_call(functools.partial(kernel, xn=xn), grid_spec=pltpu.Prefetch...  85.4 us
    all_to_all x2, blocking collectives, to_owner(): return lax.all_to_all(flat, ('dp', 'pencil'), 0, 0, tiled=True)  63.1 us
    all_to_all x2, waiting for transfers between devices, from_owner(): lax.all_to_all(sent.reshape(dp * pencil, owned, 2 * ch), ('dp', 'pencil')...  50.5 us
    pallas_call x1, Pallas kernels, body(): pl.pallas_call(functools.partial(adjoint_kernel, total=owned, **sizes), g...  9.49 us
    all_to_all x2, starting transfers between devices, from_owner(): lax.all_to_all(sent.reshape(dp * pencil, owned, 2 * ch), ('dp', 'pencil')...  6.3 us
  transfers between devices with their start and end apart: 2, of which 2 were waited for; matrix products, arithmetic and copies ran while one was open for 1% of the time, Pallas kernels for 0%

profile of v1, /device:TPU:1, one launch (start us, length us, event | category | flops | bytes accessed | tf_op | source)
XLA Modules:
  0.0 227.8 jit_solution(7468406992753217018)
XLA Ops:
  0.6 0.0 copy-start
  0.6 15.4 %field_modes.1 = bf16[8,4,2,64,128]{4,3,2,1,0:T(8,128)(2,1)} custom-call(s32[1]{0:T(128)} %bitcast.rank, bf16[16,64,64,128]{3,2,1,0:T(8,128)(2,1)} %bitcast.19, f32[2,8,8,256]{3,2,1,0:T(8,128)} %constant.14.clone.ytab, f32[2,128,256]{2,1,0:T(8,128)} %constant.15.clone.ztab, bf16[4,256,512]{2,1,0:T(8,128)(2,1)} %constant.16.clone.xf), custom_call_target="tpu_custom_call" | custom-call | tf_op jit(solution)/shard_map/field_modes/pallas_call | solution.py:302
  16.0 33.5 %all_to_all.20.received = bf16[32,128,128]{2,1,0:T(8,128)(2,1)} all-to-all(bf16[32,128,128]{2,1,0:T(8,128)(2,1)} %bitcast.27), channel_id=1, replica_groups=mesh['dp'=8,'pencil'=4] {'dp','pencil'}, dimensions={0} | all-to-all | bytes 2097152 | tf_op jit(solution)/shard_map/all_to_all | solution.py:327
  49.5 3.8 %apply_modes.1 = (f32[1024,128]{1,0:T(8,128)}, bf16[8,128,128]{2,1,0:T(8,128)(2,1)}) custom-call(bf16[32,128,128]{2,1,0:T(8,128)(2,1)} %all_to_all.20.received, bf16[128,64,128]{2,1,0:T(8,128)(2,1)} %bitcast.23), custom_call_target="tpu_custom_call" | custom-call | tf_op jit(solution)/shard_map/apply_modes/pallas_call | solution.py:351
  53.4 2.2 broadcast_in_dim.12
  55.5 3.2 %all-to-all-start.1 = ((bf16[32,128,128]{2,1,0:T(8,128)(2,1)}), bf16[32,128,128]{2,1,0:T(8,128)(2,1)S(1)}, u32[]{:S(2)}, u32[]{:S(2)}) async-start(bf16[32,128,128]{2,1,0:T(8,128)(2,1)} %bitcast.4), calls=%async_computation.1 | async-start | bytes 2097152 | tf_op jit(solution)/shard_map/all_to_all | solution.py:331
  58.7 0.0 copy-done
  58.7 0.1 copy.14
  58.8 0.3 broadcast_multiply_fusion
  59.1 0.9 mul.44.mix
  59.9 25.1 %all-to-all-done.1 = bf16[32,128,128]{2,1,0:T(8,128)(2,1)S(1)} async-done(((bf16[32,128,128]{2,1,0:T(8,128)(2,1)}), bf16[32,128,128]{2,1,0:T(8,128)(2,1)S(1)}, u32[]{:S(2)}, u32[]{:S(2)}) %all-to-all-start.1) | async-done | bytes 1048608 | tf_op jit(solution)/shard_map/all_to_all | solution.py:331
  85.0 1.0 copy.19
  86.0 45.3 %slope_modes.1 = (bf16[16,64,64,128]{3,2,1,0:T(8,128)(2,1)}, bf16[8,4,2,64,128]{4,3,2,1,0:T(8,128)(2,1)}) custom-call(s32[1]{0:T(128)} %bitcast.rank, bf16[4,8,2,64,128]{4,3,2,1,0:T(8,128)(2,1)} %bitcast.26, bf16[16,64,64,128]{3,2,1,0:T(8,128)(2,1)} %bitcast.20, bf16[16,64,64,128]{3,2,1,0:T(8,128)(2,1)} %bitcast.21, bf16[256,256]{1,0:T(8,128)(2,1)} %mul.44.mix, ...), custom_call_target="tpu_custom_call" | custom-call | tf_op jit(solution)/shard_map/slope_modes/pallas_call | solution.py:302
  131.3 29.6 %all_to_all.21.received = bf16[32,128,128]{2,1,0:T(8,128)(2,1)} all-to-all(bf16[32,128,128]{2,1,0:T(8,128)(2,1)} %bitcast.30), channel_id=1, replica_groups=mesh['dp'=8,'pencil'=4] {'dp','pencil'}, dimensions={0} | all-to-all | bytes 2097152 | tf_op jit(solution)/shard_map/all_to_all | solution.py:327
  160.9 9.5 %adjoint_modes.1 = (bf16[8,128,128]{2,1,0:T(8,128)(2,1)}, f32[128,64,128]{2,1,0:T(8,128)}) custom-call(bf16[32,128,128]{2,1,0:T(8,128)(2,1)} %all_to_all.21.received, bf16[128,64,128]{2,1,0:T(8,128)(2,1)} %bitcast.24, f32[1024,128]{1,0:T(8,128)} %get-tuple-element.10.uhat), custom_call_target="tpu_custom_call" | custom-call | tf_op jit(solution)/shard_map/adjoint_modes/pallas_call | solution.py:387
  170.4 2.2 broadcast_in_dim.22
  172.6 3.1 %all-to-all-start.3 = ((bf16[32,128,128]{2,1,0:T(8,128)(2,1)}), bf16[32,128,128]{2,1,0:T(8,128)(2,1)S(1)}, u32[]{:S(2)}, u32[]{:S(2)}) async-start(bf16[32,128,128]{2,1,0:T(8,128)(2,1)} %bitcast.10), calls=%async_computation.3 | async-start | bytes 2097152 | tf_op jit(solution)/shard_map/all_to_all | solution.py:331
  175.7 0.9 mul.47.mix
  176.6 25.4 %all-to-all-done.3 = bf16[32,128,128]{2,1,0:T(8,128)(2,1)S(1)} async-done(((bf16[32,128,128]{2,1,0:T(8,128)(2,1)}), bf16[32,128,128]{2,1,0:T(8,128)(2,1)S(1)}, u32[]{:S(2)}, u32[]{:S(2)}) %all-to-all-start.3) | async-done | bytes 1048608 | tf_op jit(solution)/shard_map/all_to_all | solution.py:331
  202.1 1.1 copy.18
  203.1 24.7 %grad_field.1 = bf16[16,64,64,128]{3,2,1,0:T(8,128)(2,1)} custom-call(s32[1]{0:T(128)} %bitcast.rank, bf16[4,8,2,64,128]{4,3,2,1,0:T(8,128)(2,1)} %bitcast.25, bf16[16,64,64,128]{3,2,1,0:T(8,128)(2,1)} %get-tuple-element.12.slope, bf16[256,256]{1,0:T(8,128)(2,1)} %mul.47.mix, f32[2,16,4,256]{3,2,1,0:T(4,128)} %constant.17.clone.ytab, ...), custom_call_target="tpu_custom_call" | custom-call | tf_op jit(solution)/shard_map/grad_field/pallas_call | solution.py:302
  (1 shorter events, 0.0 us)
Async XLA Ops:
  0.6 58.0 %copy-start = (bf16[64,64]{1,0:T(8,128)(2,1)S(1)}, bf16[64,64]{1,0:T(8,128)(2,1)}, u32[]{:S(2)}) copy-start(bf16[64,64]{1,0:T(8,128)(2,1)} %param.13) | copy-start | bytes 24580
  55.5 29.5 %all-to-all-start.1 = ((bf16[32,128,128]{2,1,0:T(8,128)(2,1)}), bf16[32,128,128]{2,1,0:T(8,128)(2,1)S(1)}, u32[]{:S(2)}, u32[]{:S(2)}) async-start(bf16[32,128,128]{2,1,0:T(8,128)(2,1)} %bitcast.4), calls=%async_computation.1 | async-start | bytes 2097152 | tf_op jit(solution)/shard_map/all_to_all | solution.py:331
  172.6 29.5 %all-to-all-start.3 = ((bf16[32,128,128]{2,1,0:T(8,128)(2,1)}), bf16[32,128,128]{2,1,0:T(8,128)(2,1)S(1)}, u32[]{:S(2)}, u32[]{:S(2)}) async-start(bf16[32,128,128]{2,1,0:T(8,128)(2,1)} %bitcast.10), calls=%async_computation.3 | async-start | bytes 2097152 | tf_op jit(solution)/shard_map/all_to_all | solution.py:331

commit v2 on v0

v2 whole, which is shorter than its diff:
```python
import functools
import math

import jax
import jax.numpy as jnp
import numpy as np
from jax import lax
from jax.experimental import pallas as pl
from jax.experimental.pallas import tpu as pltpu
from jax.sharding import PartitionSpec as P

F32 = jnp.float32
BF16 = jnp.bfloat16
SUB = 16
LIMIT = 60 * 1024 * 1024
BELL = 1.0 - 0.5 * math.log2(math.pi)


def phases(length, count, signed):
    position = np.arange(length)
    index = np.arange(count)
    freq = np.where(index < count // 2, index, index - count) if signed else index
    angle = np.mod(position[:, None] * freq[None, :], length) * (2.0 * math.pi / length)
    return np.cos(angle), np.sin(angle)


def kron_tables(nx, mx, parts):
    cos_x, sin_x = phases(nx, mx, True)
    eye = np.eye(SUB)
    local = nx // parts
    fwd, inv = [], []
    for p in range(parts):
        c = cos_x[p * local : (p + 1) * local]
        s = sin_x[p * local : (p + 1) * local]
        fwd.append(np.concatenate([np.kron(c.T, eye), np.kron(s.T, eye)], 1))
        inv.append(np.concatenate([np.kron(c, eye), np.kron(s, eye)], 1))
    return np.stack(fwd).astype(jnp.bfloat16), np.stack(inv).astype(jnp.bfloat16)


HALVES = 2


def grid_tables(ny, my, nz, mz, folded):
    cos_y, sin_y = phases(ny, my, True)
    cos_z, sin_z = phases(nz, mz, False)
    cos_z = cos_z.astype(jnp.bfloat16).astype(np.float32)
    sin_z = sin_z.astype(jnp.bfloat16).astype(np.float32)
    kh = mz // HALVES

    def pick(y, z, t):
        if folded:
            y = y[: ny // HALVES, t::HALVES]
        else:
            z = z[:, t * kh : (t + 1) * kh]
        return np.repeat(y, z.shape[1], 1), np.tile(z, (1, y.shape[1]))

    ytab, ztab = [], []
    for y, z in ((cos_y, cos_z), (sin_y, sin_z)):
        pairs = [pick(y, z, t) for t in range(HALVES)]
        ytab.append([p[0] for p in pairs])
        ztab.append([p[1] for p in pairs])
    return np.array(ytab, np.float32), np.array(ztab, np.float32)


def fill_basis(basis, ytab, ztab, i):
    yb = ytab.shape[3]
    nz = ztab.shape[2]
    for t in range(HALVES):
        cz = ztab[0, t]
        sz = ztab[1, t]
        for y in range(yb):
            cy = ytab[0, t, i, y : y + 1, :]
            sy = ytab[1, t, i, y : y + 1, :]
            re = cy * cz - sy * sz
            im = -(sy * cz + cy * sz)
            basis[t][y * nz : (y + 1) * nz, :] = jnp.concatenate([re, im], 1).astype(BF16)


def x_forward_store(acc, xf, out, mx):
    xl, ch, wide = acc[0].shape
    kept = wide // 2
    parts = []
    for g in range(ch // SUB):
        sides = []
        for t in range(HALVES):
            a = acc[t][:, g * SUB : (g + 1) * SUB, :].reshape(xl * SUB, wide).astype(BF16)
            re = a[:, :kept]
            im = a[:, kept:]
            sides.append(
                jnp.concatenate(
                    [jnp.concatenate([re, im], 1), jnp.concatenate([im, -re], 1)], 0
                )
            )
        rhs = jnp.concatenate(sides, 1)
        parts.append(jnp.dot(xf, rhs, preferred_element_type=F32))
    dp, pencil, jo, mo, _ = out.shape
    for j in range(mx):
        rows = slice(j * SUB, (j + 1) * SUB)
        pieces = [
            part[rows, n * kept : (n + 1) * kept] for n in range(2 * HALVES) for part in parts
        ]
        turned = jnp.concatenate(pieces, 0).T.astype(BF16)
        for q in range(pencil):
            out[j // jo, q, j % jo] = turned[q * mo : (q + 1) * mo, :]


def x_inverse_load(spec, turned, xi, half, jo, pencil):
    xl, ch, wide = half[0].shape
    mx = turned.shape[0]
    mo = spec.shape[1] // jo
    for j in range(mx):
        first = (j // jo) * pencil
        rows = slice((j % jo) * mo, (j % jo + 1) * mo)
        block = jnp.concatenate([spec[first + q, rows] for q in range(pencil)], 0)
        turned[j] = block.astype(F32).T.astype(BF16)
    for g in range(ch // SUB):
        sides = []
        for t in range(HALVES):
            re, im = [
                turned[:, n * ch + g * SUB : n * ch + (g + 1) * SUB, :].reshape(
                    mx * SUB, wide // 2
                )
                for n in (2 * t, 2 * t + 1)
            ]
            sides.append(
                jnp.concatenate(
                    [jnp.concatenate([re, im], 1), jnp.concatenate([-im, re], 1)], 0
                )
            )
        b = jnp.dot(xi, jnp.concatenate(sides, 1), preferred_element_type=F32)
        for t in range(HALVES):
            half[t][:, g * SUB : (g + 1) * SUB, :] = (
                b[:, t * wide : (t + 1) * wide].reshape(xl, SUB, wide).astype(BF16)
            )


def grid_rows(ref, x0, xn, yb):
    ch, nz = ref.shape[2], ref.shape[3]
    return jnp.concatenate(
        [ref[x0 : x0 + xn, y].reshape(xn * ch, nz) for y in range(yb)], 1
    )


def mixed(mix, ref, x0, xn, yb):
    per = mix.shape[1] // ref.shape[2]
    table = mix[...]
    return jnp.concatenate(
        [
            jnp.dot(table, grid_rows(ref, x, per, yb), preferred_element_type=F32)
            for x in range(x0, x0 + xn, per)
        ],
        0,
    )


def forward_sums(values, basis, acc, x0, xn):
    ch = acc[0].shape[1]
    if len(values) == 2:
        sides = (values[0] + values[1], values[0] - values[1])
    else:
        sides = (values[0], values[0])
    for t in range(HALVES):
        part = jnp.dot(sides[t], basis[t][...], preferred_element_type=F32)
        acc[t][x0 : x0 + xn] += part.reshape(xn, ch, part.shape[1])


def inverse_sums(half, basis, x0, xn, count):
    sides = []
    for t in range(HALVES):
        rows = half[t][x0 : x0 + xn]
        rows = rows.reshape(xn * rows.shape[1], rows.shape[2])
        sides.append(
            lax.dot_general(
                rows, basis[t][...], (((1,), (1,)), ((), ())), preferred_element_type=F32
            )
        )
    if count == 2:
        return [sides[0] + sides[1], sides[0] - sides[1]]
    return [sides[0] + sides[1]]


def block_copies(src, dst, sems, row, first):
    _, _, yb, chans, _ = dst.shape

    def one(i):
        return pltpu.make_async_copy(
            src.at[:, pl.ds(i * yb, yb), pl.ds(first, chans)], dst.at[i], sems.at[row, i]
        )

    return one


def step_blocks(i, steps, blocks):
    return [i + n * steps for n in range(blocks // steps)]


AHEAD = 2


def start_first(steps, blocks, loads):
    for i in range(min(AHEAD, steps)):
        for b in step_blocks(i, steps, blocks):
            for load in loads:
                load(b).start()


def start_next(i, steps, blocks, loads):
    @pl.when(i + AHEAD < steps)
    def _():
        for b in step_blocks(i + AHEAD, steps, blocks):
            for load in loads:
                load(b).start()


def forward_kernel(
    rank, field, ytab, ztab, xf, out, b0, b1, a0, a1, fbuf, sems, *, xn, jo, first
):
    basis, acc = (b0, b1), (a0, a1)
    blocks, xl, yb, ch, nz = fbuf.shape
    steps = ytab.shape[2]
    load = block_copies(field, fbuf, sems, 0, first)
    start_first(steps, blocks, [load])
    for part in acc:
        part[...] = jnp.zeros_like(part)

    def step(i, carry):
        fill_basis(basis, ytab, ztab, i)
        held = step_blocks(i, steps, blocks)
        start_next(i, steps, blocks, [load])
        for b in held:
            load(b).wait()
        for x0 in range(0, xl, xn):
            values = [grid_rows(fbuf.at[b], x0, xn, yb) for b in held]
            forward_sums(values, basis, acc, x0, xn)
        return carry

    lax.fori_loop(0, steps, step, 0)
    x_forward_store(acc, xf[0], out, xf.shape[1] // SUB)


def slope_kernel(rank, spec, mix, ytab, ztab, xf, xi, field, cot, *rest, xn, jo, first):
    slope, out, b0, b1, a0, a1, turned, h0, h1, fbuf, cbuf, sems = rest[-12:]
    basis, acc, half = (b0, b1), (a0, a1), (h0, h1)
    blocks, xl, yb, ch, nz = cbuf.shape
    steps = ytab.shape[2]
    load_f = block_copies(field, fbuf, sems, 0, 0)
    load_c = block_copies(cot, cbuf, sems, 1, first)
    start_first(steps, blocks, [load_f, load_c])

    def store(b):
        return pltpu.make_async_copy(
            cbuf.at[b], slope.at[:, pl.ds(b * yb, yb), pl.ds(first, ch)], sems.at[2, b]
        )

    for part in acc:
        part[...] = jnp.zeros_like(part)
    x_inverse_load(spec, turned, xi[0], half, jo, out.shape[1])

    def step(i, carry):
        fill_basis(basis, ytab, ztab, i)
        held = step_blocks(i, steps, blocks)
        start_next(i, steps, blocks, [load_f, load_c])
        for b in held:
            load_f(b).wait()
            load_c(b).wait()
        starts = list(range(0, xl, xn))

        def before(x0):
            grid = inverse_sums(half, basis, x0, xn, len(held))
            return [
                pre + mixed(mix, fbuf.at[b], x0, xn, yb) for b, pre in zip(held, grid)
            ]

        ahead = before(starts[0])
        for n, x0 in enumerate(starts):
            grid = ahead
            if n + 1 < len(starts):
                ahead = before(starts[n + 1])
            values = []
            for b, pre in zip(held, grid):
                cot_b = cbuf.at[b]
                q = pre * (1.0 / math.sqrt(2.0))
                bell = jnp.exp2(q * q * (-math.log2(math.e)) + BELL) * q
                gain = (1.0 + lax.erf(q)) + bell
                value = grid_rows(cot_b, x0, xn, yb) * gain.astype(BF16)
                for y in range(yb):
                    cot_b[x0 : x0 + xn, y] = value[:, y * nz : (y + 1) * nz].reshape(xn, ch, nz)
                values.append(value)
            forward_sums(values, basis, acc, x0, xn)
        for b in held:
            store(b).start()
        return carry

    lax.fori_loop(0, steps, step, 0)
    x_forward_store(acc, xf[0], out, xf.shape[1] // SUB)
    for b in range(blocks):
        store(b).wait()


def inverse_kernel(rank, spec, mix, ytab, ztab, xi, slope, *rest, xn, jo, pencil, first):
    grad, b0, b1, turned, h0, h1, sbuf, gbuf, sems = rest[-9:]
    basis, half = (b0, b1), (h0, h1)
    blocks, xl, yb, ch, nz = gbuf.shape
    steps = ytab.shape[2]
    load = block_copies(slope, sbuf, sems, 0, 0)
    start_first(steps, blocks, [load])

    def store(b):
        return pltpu.make_async_copy(
            gbuf.at[b], grad.at[:, pl.ds(b * yb, yb), pl.ds(first, ch)], sems.at[1, b]
        )

    x_inverse_load(spec, turned, xi[0], half, jo, pencil)

    def step(i, carry):
        fill_basis(basis, ytab, ztab, i)
        held = step_blocks(i, steps, blocks)
        start_next(i, steps, blocks, [load])
        for b in held:
            load(b).wait()
        starts = list(range(0, xl, xn))

        def before(x0):
            grid = inverse_sums(half, basis, x0, xn, len(held))
            return [(mixed(mix, sbuf.at[b], x0, xn, yb), g) for b, g in zip(held, grid)]

        ahead = before(starts[0])
        for n, x0 in enumerate(starts):
            grid = ahead
            if n + 1 < len(starts):
                ahead = before(starts[n + 1])
            for b, (spread, total) in zip(held, grid):
                out_b = gbuf.at[b]
                total = (total + spread).astype(BF16)
                for y in range(yb):
                    out_b[x0 : x0 + xn, y] = total[:, y * nz : (y + 1) * nz].reshape(xn, ch, nz)
        for b in held:
            store(b).start()
        return carry

    lax.fori_loop(0, steps, step, 0)
    for b in range(blocks):
        store(b).wait()


def lane(rows, wide):
    return lax.broadcasted_iota(jnp.int32, (rows, wide), 1)


def gather_partials(received, store, pencil, scale):
    modes = received.shape[1]
    for s in range(received.shape[0] // pencil):
        total = received[s * pencil].astype(F32)
        for p in range(1, pencil):
            total = total + received[s * pencil + p].astype(F32)
        store[s * modes : (s + 1) * modes, :] = (total * scale).astype(BF16).astype(F32)


def unpack(a, b):
    rows, wide = a.shape
    quarter = wide // (2 * HALVES)
    even = (lane(rows, wide) // quarter) % 2 == 0
    re = jnp.where(even, a, pltpu.roll(b, quarter, 1))
    im = jnp.where(even, pltpu.roll(a, wide - quarter, 1), b)
    return re, im


def pack(re, im):
    rows, wide = re.shape
    quarter = wide // (2 * HALVES)
    even = (lane(rows, wide) // quarter) % 2 == 0
    a = jnp.where(even, re, pltpu.roll(im, quarter, 1))
    b = jnp.where(even, pltpu.roll(re, wide - quarter, 1), im)
    return a, b


def swap(values):
    return pltpu.roll(values, values.shape[-1] // 2, 1)


def every(outer, inner, step):
    def body(o, carry):
        for i in range(inner):
            step(o, i)
        return carry

    lax.fori_loop(0, outer, body, 0)


def apply_kernel(got_a, got_b, weights, out_a, out_b, masked, ua, ub, va, vb, *, pencil, size, folded):
    outer, halves, kh, ch, wide = weights.shape
    samples = got_a.shape[0] // pencil
    total = got_a.shape[1]
    gather_partials(got_a, ua, pencil, 1.0)
    gather_partials(got_b, ub, pencil, 1.0)

    low = lane(samples, wide) < ch
    sign = jnp.where(low, -1.0, 1.0).astype(F32)
    zero = jnp.zeros((samples, wide), F32)

    def step(o, i):
        rows = pl.ds(o * kh + i, samples, stride=total)
        re, im = unpack(ua[rows, :], ub[rows, :])
        lhs = jnp.concatenate(
            [
                jnp.where(low, re, zero),
                jnp.where(low, im, zero),
                jnp.where(low, zero, re),
                jnp.where(low, zero, im),
            ],
            0,
        ).astype(BF16)
        masked[o * kh + i] = lhs
        rhs = jnp.concatenate([weights[o, 0, i], weights[o, 1, i]], 0)
        got = jnp.dot(lhs, rhs, preferred_element_type=F32)
        v0 = got[:samples] + sign * swap(got[samples : 2 * samples])
        v1 = got[2 * samples : 3 * samples] + sign * swap(got[3 * samples :])
        a, b = pack(jnp.where(low, v0, swap(v1)), jnp.where(low, swap(v0), v1))
        va[rows, :] = a
        vb[rows, :] = b

    every(outer, kh, step)
    scale = mode_scale(total, wide, kh, size, folded)
    for s in range(samples):
        for v, out in ((va, out_a), (vb, out_b)):
            value = (v[s * total : (s + 1) * total, :] * scale).astype(BF16)
            for p in range(pencil):
                out[s * pencil + p] = value


def mode_scale(modes, wide, kh, size, folded):
    first = lax.broadcasted_iota(jnp.int32, (modes, wide), 0) % kh == 0
    if not folded:
        first = first & (lane(modes, wide) < wide // HALVES)
    return jnp.where(first, 1.0 / size, 2.0 / size).astype(F32)


def adjoint_kernel(got_a, got_b, weights, out_a, out_b, stacked, ga, gb, va, vb, *, pencil, size, folded):
    outer, halves, kh, ch, wide = weights.shape
    samples = got_a.shape[0] // pencil
    total = got_a.shape[1]
    scale = 0.5 * mode_scale(total, wide, kh, size, folded)
    gather_partials(got_a, ga, pencil, scale)
    gather_partials(got_b, gb, pencil, scale)

    low = lane(samples, wide) < ch

    def step(o, i):
        rows = pl.ds(o * kh + i, samples, stride=total)
        re, im = unpack(ga[rows, :], gb[rows, :])
        er, mi = swap(re), swap(im)
        lhs = jnp.concatenate(
            [
                jnp.where(low, re, mi),
                jnp.where(low, im, -er),
                jnp.where(low, er, im),
                jnp.where(low, mi, -re),
            ],
            0,
        ).astype(BF16)
        stacked[o * kh + i] = lhs
        rhs = jnp.concatenate([weights[o, 0, i], weights[o, 1, i]], 0)
        got = lax.dot_general(
            lhs, rhs, (((1,), (1,)), ((), ())), preferred_element_type=F32
        )
        a, b = pack(
            jnp.where(low, got[:samples], got[2 * samples : 3 * samples]),
            jnp.where(low, got[samples : 2 * samples], got[3 * samples :]),
        )
        va[rows, :] = a
        vb[rows, :] = b

    every(outer, kh, step)
    for s in range(samples):
        for v, out in ((va, out_a), (vb, out_b)):
            value = v[s * total : (s + 1) * total, :].astype(BF16)
            for p in range(pencil):
                out[s * pencil + p] = value


def grads_kernel(masked, stacked, grad):
    kh, _, wide = masked.shape
    for i in range(kh):
        both = lax.dot_general(
            masked[i], stacked[i], (((0,), (0,)), ((), ())), preferred_element_type=F32
        )
        grad[0, 0, i] = both[: wide // 2]
        grad[0, 1, i] = both[wide // 2 :]


def params():
    return pltpu.CompilerParams(dimension_semantics=("arbitrary",), vmem_limit_bytes=LIMIT)


def whole(shape):
    return pl.BlockSpec(shape, lambda i, *r: (0,) * len(shape))


def make_body(dp, pencil):
    def body(field, cotangent, w_spec, w_local):
        sample = field[0]
        target = cotangent[0]
        xl, ny, ch, nz = sample.shape
        jo, lo, mz, _, wide = w_spec.shape
        nx, mx, my = xl * pencil, jo * dp, lo * pencil
        modes = my * mz
        folded = lo % HALVES == 0
        kh = mz if folded else mz // HALVES
        outer = jo * lo * mz // (HALVES * kh)
        hc = ch // HALVES
        owned = outer * kh
        size = nx * ny * nz
        xn = min(xl, 8)
        per = min(xl, 4)
        rank = lax.axis_index("pencil").astype(jnp.int32).reshape(1)

        xf, xi = kron_tables(nx, mx, pencil)
        ytab, ztab = grid_tables(ny, my, nz, mz, folded)
        weights = w_spec.reshape(outer, HALVES, kh, ch, wide)
        eye = jnp.eye(per, dtype=BF16)
        mix_out = [jnp.kron(eye, w_local[:, h * hc : (h + 1) * hc].T) for h in range(HALVES)]
        halved = w_local * jnp.asarray(0.5, BF16)
        mix_in = [jnp.kron(eye, halved[h * hc : (h + 1) * hc]) for h in range(HALVES)]

        def y_spec(yb):
            return whole(y_table(yb).shape)

        def y_table(yb):
            return ytab.reshape(2, HALVES, -1, yb, ytab.shape[-1])

        def held(yb, channels):
            return pltpu.VMEM((ny // yb, xl, yb, channels, nz), BF16)

        def sems(rows, yb):
            return pltpu.SemaphoreType.DMA((rows, ny // yb))

        z_spec = whole(ztab.shape)
        ranked = lambda t: pl.BlockSpec((1,) + t.shape[1:], lambda i, r: (r[0], 0, 0))
        anywhere = pl.BlockSpec(memory_space=pl.ANY)
        packed = (dp, pencil, jo, owned // jo, wide)
        flat = (dp * pencil, owned, wide)

        def call(kernel, yb, ins, outs, shapes, scratch, name, args, flops, alias=None):
            aliases = {}
            if alias is not None:
                ins = ins + [anywhere]
                args = args + (alias,)
                aliases = {len(args): 0}
            return pl.pallas_call(
                kernel,
                grid_spec=pltpu.PrefetchScalarGridSpec(
                    num_scalar_prefetch=1,
                    grid=(1,),
                    in_specs=ins,
                    out_specs=outs,
                    scratch_shapes=scratch,
                ),
                out_shape=shapes,
                input_output_aliases=aliases,
                compiler_params=params(),
                cost_estimate=pl.CostEstimate(
                    flops=flops, bytes_accessed=2 * sample.size, transcendentals=0
                ),
                name=name,
            )(rank, *args)

        def basis(yb):
            return [pltpu.VMEM((yb * nz, modes), BF16)] * HALVES

        acc = [pltpu.VMEM((xl, hc, modes), F32)] * HALVES
        turned = pltpu.VMEM((mx, wide, modes // HALVES), BF16)
        half = [pltpu.VMEM((xl, hc, modes), BF16)] * HALVES
        spectrum = jax.ShapeDtypeStruct(packed, BF16)
        grid_shape = jax.ShapeDtypeStruct(sample.shape, BF16)
        work = 2 * xl * hc * ny * nz * 2 * modes

        def exchange(values):
            return lax.all_to_all(values.reshape(flat), ("dp", "pencil"), 0, 0, tiled=True)

        def owner_call(kernel, args, ins, outs, shapes, scratch, name, steps=1):
            return pl.pallas_call(
                kernel,
                grid=(steps,),
                in_specs=ins,
                out_specs=outs,
                out_shape=shapes,
                scratch_shapes=scratch,
                compiler_params=params(),
                cost_estimate=pl.CostEstimate(
                    flops=work // 4, bytes_accessed=w_spec.size * 2, transcendentals=0
                ),
                name=name,
            )(*args)

        samples = dp
        moving = pl.BlockSpec((1, HALVES, kh, ch, wide), lambda i: (i, 0, 0, 0, 0))
        lines = pl.BlockSpec((kh, 4 * samples, wide), lambda i: (i, 0, 0))
        line_shape = jax.ShapeDtypeStruct((owned, 4 * samples, wide), BF16)
        message = jax.ShapeDtypeStruct(flat, BF16)
        store = pltpu.VMEM((samples * owned, wide), F32)
        options = dict(pencil=pencil, size=size, folded=folded)

        yb = 8
        got = []
        for h in range(HALVES):
            modes_h = call(
                functools.partial(forward_kernel, xn=xn, jo=jo, first=h * hc),
                yb,
                [anywhere, y_spec(yb), z_spec, ranked(xf)],
                whole(packed),
                spectrum,
                [*basis(yb), *acc, held(yb, hc), sems(1, yb)],
                "field_modes_%d" % h,
                (sample, y_table(yb), ztab, xf),
                work,
            )
            if got:
                modes_h, got[0] = lax.optimization_barrier((modes_h, got[0]))
            got.append(exchange(modes_h))
        va, vb, masked = owner_call(
            functools.partial(apply_kernel, **options),
            (got[0], got[1], weights),
            [whole(flat), whole(flat), whole(weights.shape)],
            (whole(flat), whole(flat), whole(line_shape.shape)),
            (message, message, line_shape),
            [store] * 4,
            "apply_modes",
        )
        spec = [exchange(va), exchange(vb)]
        yb = 4
        slope = None
        got = []
        for h in range(HALVES):
            slope, modes_h = call(
                functools.partial(slope_kernel, xn=xn, jo=jo, first=h * hc),
                yb,
                [
                    whole(flat),
                    whole(mix_out[h].shape),
                    y_spec(yb),
                    z_spec,
                    ranked(xf),
                    ranked(xi),
                    anywhere,
                    anywhere,
                ],
                (anywhere, whole(packed)),
                (grid_shape, spectrum),
                [*basis(yb), *acc, turned, *half, held(yb, ch), held(yb, hc), sems(3, yb)],
                "slope_modes_%d" % h,
                (spec[h], mix_out[h], y_table(yb), ztab, xf, xi, sample, target),
                3 * work,
                slope,
            )
            if got:
                modes_h, got[0] = lax.optimization_barrier((modes_h, got[0]))
            got.append(exchange(modes_h))
        da, db, stacked = owner_call(
            functools.partial(adjoint_kernel, **options),
            (got[0], got[1], weights),
            [whole(flat), whole(flat), whole(weights.shape)],
            (whole(flat), whole(flat), whole(line_shape.shape)),
            (message, message, line_shape),
            [store] * 4,
            "adjoint_modes",
        )
        spec = [exchange(da)]
        grad_w = owner_call(
            grads_kernel,
            (masked, stacked),
            [lines, lines],
            moving,
            jax.ShapeDtypeStruct(weights.shape, F32),
            [],
            "weight_grads",
            outer,
        )
        db, spec[0], grad_w, mix_in = lax.optimization_barrier((db, spec[0], grad_w, mix_in))
        spec.append(exchange(db))
        grad = None
        for h in range(HALVES):
            grad = call(
                functools.partial(inverse_kernel, xn=xn, jo=jo, pencil=pencil, first=h * hc),
                yb,
                [
                    whole(flat),
                    whole(mix_in[h].shape),
                    y_spec(yb),
                    z_spec,
                    ranked(xi),
                    anywhere,
                ],
                anywhere,
                grid_shape,
                [*basis(yb), turned, *half, held(yb, ch), held(yb, hc), sems(2, yb)],
                "grad_field_%d" % h,
                (spec[h], mix_in[h], y_table(yb), ztab, xi, slope),
                2 * work,
                grad,
            )
        return grad[None], grad_w.reshape(w_spec.shape)

    return body


def solution(mesh):
    split = P("dp", "pencil", None, None, None)
    return jax.shard_map(
        make_body(mesh.shape["dp"], mesh.shape["pencil"]),
        mesh=mesh,
        in_specs=(split, split, split, P()),
        out_specs=(split, split),
        check_vma=False,
    )
```

time: 630 us -> 202 us (0.32)
  matrix products: 370 us -> 0 us
  Pallas kernels: 0 us -> 97.1 us
  local copies, waits for them, and re-layouts: 63 us -> 4.11 us
  other arithmetic: 38.9 us -> 0.28 us
  waiting for transfers between devices: 70.6 us -> 33.2 us
  blocking collectives: 69.3 us -> 39.8 us
  starting transfers between devices: 11.6 us -> 25.6 us
    dot_general x28 -> x0, matrix products: 370 us -> none  [the longest x2 130 us: z_back(): jnp.dot(values.reshape(-1, shape_in[-1]), matrix, precision=HIGHEST, pref...]
    pallas_call x0 -> x9, Pallas kernels: none -> 97.1 us  [the longest x6 81.2 us: call(): pl.pallas_call(kernel, grid_spec=pltpu.PrefetchScalarGridSpec(num_scalar_...]
    all_to_all x3 -> x6, waiting for transfers between devices: 70.6 us -> 33.2 us  [exchange(): lax.all_to_all(values.reshape(flat), ('dp', 'pencil'), 0, 0, tiled=True)]
    unnamed x41 -> x14, local copies, waits for them, and re-layouts: 32 us -> 0.83 us
    all_to_all x5 -> x2, blocking collectives: 69.3 us -> 39.8 us  [exchange(): lax.all_to_all(values.reshape(flat), ('dp', 'pencil'), 0, 0, tiled=True)]
    slice x8 -> x0, other arithmetic: 22.5 us -> none  [rotate_half(): return jnp.concatenate([values[..., middle:], -values[..., :middle]], -1)]
    all_to_all x3 -> x6, starting transfers between devices: 11.6 us -> 25.6 us  [exchange(): lax.all_to_all(values.reshape(flat), ('dp', 'pencil'), 0, 0, tiled=True)]
    reshape x1 -> x0, local copies, waits for them, and re-layouts: 12.7 us -> none  [z_forward(): return product.reshape(shape_in[:-1] + (matrix.shape[1],))]
  transfers between devices with their start and end apart: 3 -> 6, of which waited for: 3 -> 4; matrix products, arithmetic and copies ran while one was open for 1% -> 2% of each run, Pallas kernels for 0% -> 33%
where the time goes in v2:
time: 202 us; the launch traced here: 201 us
  Pallas kernels  97.1 us (48%)
  blocking collectives  39.8 us (20%)
  waiting for transfers between devices  33.2 us (16%)
  starting transfers between devices  25.6 us (13%)
  local copies, waits for them, and re-layouts  4.11 us (2%)
    pallas_call x6, Pallas kernels, call(): pl.pallas_call(kernel, grid_spec=pltpu.PrefetchScalarGridSpec(num_scalar_...  81.2 us
    all_to_all x2, blocking collectives, exchange(): lax.all_to_all(values.reshape(flat), ('dp', 'pencil'), 0, 0, tiled=True)  39.8 us
    all_to_all x6, waiting for transfers between devices, exchange(): lax.all_to_all(values.reshape(flat), ('dp', 'pencil'), 0, 0, tiled=True)  33.2 us
    all_to_all x6, starting transfers between devices, exchange(): lax.all_to_all(values.reshape(flat), ('dp', 'pencil'), 0, 0, tiled=True)  25.6 us
    pallas_call x3, Pallas kernels, owner_call(): pl.pallas_call(kernel, grid=(steps,), in_specs=ins, out_specs=outs, out_s...  15.9 us
  transfers between devices with their start and end apart: 6, of which 4 were waited for; matrix products, arithmetic and copies ran while one was open for 2% of the time, Pallas kernels for 33%

profile of v2, /device:TPU:1, one launch (start us, length us, event | category | flops | bytes accessed | tf_op | source)
XLA Modules:
  0.0 201.0 jit_solution(14646508730335853785)
XLA Ops:
  0.6 7.8 %field_modes_0.1 = bf16[8,4,2,32,128]{4,3,2,1,0:T(8,128)(2,1)} custom-call(s32[1]{0:T(128)} %bitcast.rank, bf16[16,64,64,128]{3,2,1,0:T(8,128)(2,1)} %bitcast.14, f32[2,2,4,8,128]{4,3,2,1,0:T(8,128)} %constant.16.clone.ytab, f32[2,2,128,128]{3,2,1,0:T(8,128)} %constant.17.clone.ztab, bf16[4,256,512]{2,1,0:T(8,128)(2,1)} %constant.18.clone.xf), custom_call_target="tpu_custom_call" | custom-call | flops 4294967296 | bytes 16777216 | tf_op jit(solution)/shard_map/field_modes_0/pallas_call | solution.py:549
  8.4 7.1 %all-to-all-start = ((bf16[32,64,128]{2,1,0:T(8,128)(2,1)}), bf16[32,64,128]{2,1,0:T(8,128)(2,1)S(1)}, u32[]{:S(2)}, u32[]{:S(2)}) async-start(bf16[32,64,128]{2,1,0:T(8,128)(2,1)} %bitcast.22), calls=%async_computation | async-start | bytes 1048576 | tf_op jit(solution)/shard_map/all_to_all | solution.py:578
  15.5 7.8 %field_modes_1.1 = bf16[8,4,2,32,128]{4,3,2,1,0:T(8,128)(2,1)} custom-call(s32[1]{0:T(128)} %bitcast.rank, bf16[16,64,64,128]{3,2,1,0:T(8,128)(2,1)} %bitcast.15, f32[2,2,4,8,128]{4,3,2,1,0:T(8,128)} %constant.16.clone.ytab, f32[2,2,128,128]{3,2,1,0:T(8,128)} %constant.17.clone.ztab, bf16[4,256,512]{2,1,0:T(8,128)(2,1)} %constant.18.clone.xf), custom_call_target="tpu_custom_call" | custom-call | flops 4294967296 | bytes 16777216 | tf_op jit(solution)/shard_map/field_modes_1/pallas_call | solution.py:549
  23.3 7.5 %all-to-all-done.got_a = bf16[32,64,128]{2,1,0:T(8,128)(2,1)S(1)} async-done(((bf16[32,64,128]{2,1,0:T(8,128)(2,1)}), bf16[32,64,128]{2,1,0:T(8,128)(2,1)S(1)}, u32[]{:S(2)}, u32[]{:S(2)}) %all-to-all-start) | async-done | bytes 524320 | tf_op jit(solution)/shard_map/all_to_all | solution.py:578
  30.8 18.5 %all_to_all.40.got_b = bf16[32,64,128]{2,1,0:T(8,128)(2,1)} all-to-all(bf16[32,64,128]{2,1,0:T(8,128)(2,1)} %bitcast.23), channel_id=1, replica_groups=mesh['dp'=8,'pencil'=4] {'dp','pencil'}, dimensions={0} | all-to-all | bytes 1048576 | tf_op jit(solution)/shard_map/all_to_all | solution.py:578
  49.3 5.5 %apply_modes.1 = (bf16[32,64,128]{2,1,0:T(8,128)(2,1)}, bf16[32,64,128]{2,1,0:T(8,128)(2,1)}, bf16[64,32,128]{2,1,0:T(8,128)(2,1)}) custom-call(bf16[32,64,128]{2,1,0:T(8,128)(2,1)} %copy-done.5, bf16[32,64,128]{2,1,0:T(8,128)(2,1)} %all_to_all.40.got_b, bf16[4,2,16,64,128]{4,3,2,1,0:T(8,128)(2,1)} %bitcast.26), custom_call_target="tpu_custom_call" | custom-call | flops 1073741824 | bytes 2097152 | tf_op jit(solution)/shard_map/apply_modes/pallas_call | solution.py:581
  54.8 3.2 %all-to-all-start.3 = ((bf16[32,64,128]{2,1,0:T(8,128)(2,1)}), bf16[32,64,128]{2,1,0:T(8,128)(2,1)S(1)}, u32[]{:S(2)}, u32[]{:S(2)}) async-start(bf16[32,64,128]{2,1,0:T(8,128)(2,1)} %get-tuple-element.24), calls=%async_computation.3 | async-start | bytes 1048576 | tf_op jit(solution)/shard_map/all_to_all | solution.py:578
  59.3 0.8 mul.84.mix
  60.1 13.2 %all-to-all-done.3.spec = bf16[32,64,128]{2,1,0:T(8,128)(2,1)S(1)} async-done(((bf16[32,64,128]{2,1,0:T(8,128)(2,1)}), bf16[32,64,128]{2,1,0:T(8,128)(2,1)S(1)}, u32[]{:S(2)}, u32[]{:S(2)}) %all-to-all-start.3) | async-done | bytes 524320 | tf_op jit(solution)/shard_map/all_to_all | solution.py:578
  73.3 3.2 %all-to-all-start.2 = ((bf16[32,64,128]{2,1,0:T(8,128)(2,1)}), bf16[32,64,128]{2,1,0:T(8,128)(2,1)S(1)}, u32[]{:S(2)}, u32[]{:S(2)}) async-start(bf16[32,64,128]{2,1,0:T(8,128)(2,1)} %get-tuple-element.23), calls=%async_computation.2 | async-start | bytes 1048576 | tf_op jit(solution)/shard_map/all_to_all | solution.py:578
  76.4 21.0 %slope_modes_0.1 = (bf16[16,64,64,128]{3,2,1,0:T(8,128)(2,1)}, bf16[8,4,2,32,128]{4,3,2,1,0:T(8,128)(2,1)}) custom-call(s32[1]{0:T(128)} %bitcast.rank, bf16[32,64,128]{2,1,0:T(8,128)(2,1)} %copy-done.3, bf16[128,256]{1,0:T(8,128)(2,1)} %mul.87.mix, f32[2,2,8,4,128]{4,3,2,1,0:T(4,128)} %constant.19.clone.ytab, f32[2,2,128,128]{3,2,1,0:T(8,128)} %constant.17.clone.ztab, ...), custom_call_target="tpu_custom_call" | custom-call | flops 12884901888 | bytes 16777216 | tf_op jit(solution)/shard_map/slope_modes_0/pallas_call | solution.py:549
  97.5 5.8 %all-to-all-start.4 = ((bf16[32,64,128]{2,1,0:T(8,128)(2,1)}), bf16[32,64,128]{2,1,0:T(8,128)(2,1)S(1)}, u32[]{:S(2)}, u32[]{:S(2)}) async-start(bf16[32,64,128]{2,1,0:T(8,128)(2,1)} %bitcast.24), calls=%async_computation.4 | async-start | bytes 1048576 | tf_op jit(solution)/shard_map/all_to_all | solution.py:578
  103.3 21.0 %slope_modes_1.1 = (bf16[16,64,64,128]{3,2,1,0:T(8,128)(2,1)}, bf16[8,4,2,32,128]{4,3,2,1,0:T(8,128)(2,1)}) custom-call(s32[1]{0:T(128)} %bitcast.rank, bf16[32,64,128]{2,1,0:T(8,128)(2,1)} %copy-done.1, bf16[128,256]{1,0:T(8,128)(2,1)} %mul.84.mix, f32[2,2,8,4,128]{4,3,2,1,0:T(4,128)} %constant.19.clone.ytab, ...), custom_call_target="tpu_custom_call", output_to_operand_aliasing={{0}: (9, {})} | custom-call | flops 12884901888 | bytes 16777216 | tf_op jit(solution)/shard_map/slope_modes_1/pallas_call | solution.py:549
  124.3 21.2 %all_to_all.41.got_b = bf16[32,64,128]{2,1,0:T(8,128)(2,1)} all-to-all(bf16[32,64,128]{2,1,0:T(8,128)(2,1)} %bitcast.25), channel_id=1, replica_groups=mesh['dp'=8,'pencil'=4] {'dp','pencil'}, dimensions={0} | all-to-all | bytes 1048576 | tf_op jit(solution)/shard_map/all_to_all | solution.py:578
  145.6 5.8 %adjoint_modes.1 = (bf16[32,64,128]{2,1,0:T(8,128)(2,1)}, bf16[32,64,128]{2,1,0:T(8,128)(2,1)}, bf16[64,32,128]{2,1,0:T(8,128)(2,1)}) custom-call(bf16[32,64,128]{2,1,0:T(8,128)(2,1)} %copy-done.4, bf16[32,64,128]{2,1,0:T(8,128)(2,1)} %all_to_all.41.got_b, bf16[4,2,16,64,128]{4,3,2,1,0:T(8,128)(2,1)} %bitcast.27), custom_call_target="tpu_custom_call" | custom-call | flops 1073741824 | bytes 2097152 | tf_op jit(solution)/shard_map/adjoint_modes/pallas_call | solution.py:581
  151.4 3.2 %all-to-all-start.6 = ((bf16[32,64,128]{2,1,0:T(8,128)(2,1)}), bf16[32,64,128]{2,1,0:T(8,128)(2,1)S(1)}, u32[]{:S(2)}, u32[]{:S(2)}) async-start(bf16[32,64,128]{2,1,0:T(8,128)(2,1)} %get-tuple-element.31), calls=%async_computation.6 | async-start | bytes 1048576 | tf_op jit(solution)/shard_map/all_to_all | solution.py:578
  155.3 0.8 mul.92.mix
  156.0 4.6 %weight_grads.1 = f32[4,2,16,64,128]{4,3,2,1,0:T(8,128)} custom-call(bf16[64,32,128]{2,1,0:T(8,128)(2,1)} %get-tuple-element.32.masked, bf16[64,32,128]{2,1,0:T(8,128)(2,1)} %get-tuple-element.33.stacked), custom_call_target="tpu_custom_call" | custom-call | flops 1073741824 | bytes 2097152 | tf_op jit(solution)/shard_map/weight_grads/pallas_call | solution.py:581
  160.6 9.1 %all-to-all-done.6.spec = bf16[32,64,128]{2,1,0:T(8,128)(2,1)S(1)} async-done(((bf16[32,64,128]{2,1,0:T(8,128)(2,1)}), bf16[32,64,128]{2,1,0:T(8,128)(2,1)S(1)}, u32[]{:S(2)}, u32[]{:S(2)}) %all-to-all-start.6) | async-done | bytes 524320 | tf_op jit(solution)/shard_map/all_to_all | solution.py:578
  169.8 3.2 %all-to-all-start.7 = ((bf16[32,64,128]{2,1,0:T(8,128)(2,1)}), bf16[32,64,128]{2,1,0:T(8,128)(2,1)S(1)}, u32[]{:S(2)}, u32[]{:S(2)}) async-start(bf16[32,64,128]{2,1,0:T(8,128)(2,1)} %get-tuple-element.34), calls=%async_computation.7 | async-start | bytes 1048576 | tf_op jit(solution)/shard_map/all_to_all | solution.py:578
  173.0 11.9 %grad_field_0.1.rest_0_ = bf16[16,64,64,128]{3,2,1,0:T(8,128)(2,1)} custom-call(s32[1]{0:T(128)} %bitcast.rank, bf16[32,64,128]{2,1,0:T(8,128)(2,1)} %copy-done, bf16[128,256]{1,0:T(8,128)(2,1)} %mul.92.mix, f32[2,2,8,4,128]{4,3,2,1,0:T(4,128)} %constant.19.clone.ytab, f32[2,2,128,128]{3,2,1,0:T(8,128)} %constant.17.clone.ztab, ...), custom_call_target="tpu_custom_call" | custom-call | flops 8589934592 | bytes 16777216 | tf_op jit(solution)/shard_map/grad_field_0/pallas_call | solution.py:549
  184.8 3.4 %all-to-all-done.7.spec = bf16[32,64,128]{2,1,0:T(8,128)(2,1)S(1)} async-done(((bf16[32,64,128]{2,1,0:T(8,128)(2,1)}), bf16[32,64,128]{2,1,0:T(8,128)(2,1)S(1)}, u32[]{:S(2)}, u32[]{:S(2)}) %all-to-all-start.7) | async-done | bytes 524320 | tf_op jit(solution)/shard_map/all_to_all | solution.py:578
  188.2 0.8 copy-done.2
  189.0 11.8 %grad_field_1.1 = bf16[16,64,64,128]{3,2,1,0:T(8,128)(2,1)} custom-call(s32[1]{0:T(128)} %bitcast.rank, bf16[32,64,128]{2,1,0:T(8,128)(2,1)} %copy-done.2, bf16[128,256]{1,0:T(8,128)(2,1)} %mul.95.mix, f32[2,2,8,4,128]{4,3,2,1,0:T(4,128)} %constant.19.clone.ytab, f32[2,2,128,128]{3,2,1,0:T(8,128)} %constant.17.clone.ztab, ...), custom_call_target="tpu_custom_call", output_to_operand_aliasing={{}: (7, {})} | custom-call | flops 8589934592 | bytes 16777216 | tf_op jit(solution)/shard_map/grad_field_1/pallas_call | solution.py:549
  (24 shorter events, 2.1 us)
Async XLA Ops:
  8.4 49.6 %copy-start.6 = (bf16[64,64]{1,0:T(8,128)(2,1)S(1)}, bf16[64,64]{1,0:T(8,128)(2,1)}, u32[]{:S(2)}) copy-start(bf16[64,64]{1,0:T(8,128)(2,1)} %param.16) | copy-start | bytes 24580
  8.4 22.4 %all-to-all-start = ((bf16[32,64,128]{2,1,0:T(8,128)(2,1)}), bf16[32,64,128]{2,1,0:T(8,128)(2,1)S(1)}, u32[]{:S(2)}, u32[]{:S(2)}) async-start(bf16[32,64,128]{2,1,0:T(8,128)(2,1)} %bitcast.22), calls=%async_computation | async-start | bytes 1048576 | tf_op jit(solution)/shard_map/all_to_all | solution.py:578
  30.8 18.5 %copy-start.5 = (bf16[32,64,128]{2,1,0:T(8,128)(2,1)}, bf16[32,64,128]{2,1,0:T(8,128)(2,1)S(1)}, u32[]{:S(2)}) copy-start(bf16[32,64,128]{2,1,0:T(8,128)(2,1)S(1)} %all-to-all-done.got_a) | copy-start | bytes 1572868
  54.8 18.4 %all-to-all-start.3 = ((bf16[32,64,128]{2,1,0:T(8,128)(2,1)}), bf16[32,64,128]{2,1,0:T(8,128)(2,1)S(1)}, u32[]{:S(2)}, u32[]{:S(2)}) async-start(bf16[32,64,128]{2,1,0:T(8,128)(2,1)} %get-tuple-element.24), calls=%async_computation.3 | async-start | bytes 1048576 | tf_op jit(solution)/shard_map/all_to_all | solution.py:578
  73.3 3.2 %copy-start.3 = (bf16[32,64,128]{2,1,0:T(8,128)(2,1)}, bf16[32,64,128]{2,1,0:T(8,128)(2,1)S(1)}, u32[]{:S(2)}) copy-start(bf16[32,64,128]{2,1,0:T(8,128)(2,1)S(1)} %all-to-all-done.3.spec) | copy-start | bytes 1572868
  73.3 24.2 %all-to-all-start.2 = ((bf16[32,64,128]{2,1,0:T(8,128)(2,1)}), bf16[32,64,128]{2,1,0:T(8,128)(2,1)S(1)}, u32[]{:S(2)}, u32[]{:S(2)}) async-start(bf16[32,64,128]{2,1,0:T(8,128)(2,1)} %get-tuple-element.23), calls=%async_computation.2 | async-start | bytes 1048576 | tf_op jit(solution)/shard_map/all_to_all | solution.py:578
  97.4 5.9 %copy-start.1 = (bf16[32,64,128]{2,1,0:T(8,128)(2,1)}, bf16[32,64,128]{2,1,0:T(8,128)(2,1)S(1)}, u32[]{:S(2)}) copy-start(bf16[32,64,128]{2,1,0:T(8,128)(2,1)S(1)} %all-to-all-done.2.spec) | copy-start | bytes 1572868
  97.5 26.9 %all-to-all-start.4 = ((bf16[32,64,128]{2,1,0:T(8,128)(2,1)}), bf16[32,64,128]{2,1,0:T(8,128)(2,1)S(1)}, u32[]{:S(2)}, u32[]{:S(2)}) async-start(bf16[32,64,128]{2,1,0:T(8,128)(2,1)} %bitcast.24), calls=%async_computation.4 | async-start | bytes 1048576 | tf_op jit(solution)/shard_map/all_to_all | solution.py:578
  124.3 21.2 %copy-start.4 = (bf16[32,64,128]{2,1,0:T(8,128)(2,1)}, bf16[32,64,128]{2,1,0:T(8,128)(2,1)S(1)}, u32[]{:S(2)}) copy-start(bf16[32,64,128]{2,1,0:T(8,128)(2,1)S(1)} %all-to-all-done.4.got_a) | copy-start | bytes 1572868
  151.4 18.4 %all-to-all-start.6 = ((bf16[32,64,128]{2,1,0:T(8,128)(2,1)}), bf16[32,64,128]{2,1,0:T(8,128)(2,1)S(1)}, u32[]{:S(2)}, u32[]{:S(2)}) async-start(bf16[32,64,128]{2,1,0:T(8,128)(2,1)} %get-tuple-element.31), calls=%async_computation.6 | async-start | bytes 1048576 | tf_op jit(solution)/shard_map/all_to_all | solution.py:578
  169.8 3.2 %copy-start = (bf16[32,64,128]{2,1,0:T(8,128)(2,1)}, bf16[32,64,128]{2,1,0:T(8,128)(2,1)S(1)}, u32[]{:S(2)}) copy-start(bf16[32,64,128]{2,1,0:T(8,128)(2,1)S(1)} %all-to-all-done.6.spec) | copy-start | bytes 1572868
  169.8 18.4 %all-to-all-start.7 = ((bf16[32,64,128]{2,1,0:T(8,128)(2,1)}), bf16[32,64,128]{2,1,0:T(8,128)(2,1)S(1)}, u32[]{:S(2)}, u32[]{:S(2)}) async-start(bf16[32,64,128]{2,1,0:T(8,128)(2,1)} %get-tuple-element.34), calls=%async_computation.7 | async-start | bytes 1048576 | tf_op jit(solution)/shard_map/all_to_all | solution.py:578
  188.2 0.8 copy-start.2

commit v3 on v2

--- a/solution.py
+++ b/solution.py
@@ -13,6 +13,7 @@
 BF16 = jnp.bfloat16
 SUB = 16
 LIMIT = 60 * 1024 * 1024
+FIELD_ROWS = 4
 BELL = 1.0 - 0.5 * math.log2(math.pi)
 
 
@@ -212,30 +213,32 @@
                 load(b).start()
 
 
-def forward_kernel(
-    rank, field, ytab, ztab, xf, out, b0, b1, a0, a1, fbuf, sems, *, xn, jo, first
-):
-    basis, acc = (b0, b1), (a0, a1)
-    blocks, xl, yb, ch, nz = fbuf.shape
+def forward_kernel(rank, field, ytab, ztab, xf, out, b0, b1, *rest, xn, jo):
+    basis = (b0, b1)
+    fbuf, sems = rest[-2:]
+    acc = [rest[h * HALVES : (h + 1) * HALVES] for h in range(HALVES)]
+    _, blocks, xl, yb, ch, nz = fbuf.shape
     steps = ytab.shape[2]
-    load = block_copies(field, fbuf, sems, 0, first)
-    start_first(steps, blocks, [load])
-    for part in acc:
+    loads = [block_copies(field, fbuf.at[h], sems, h, h * ch) for h in range(HALVES)]
+    start_first(steps, blocks, loads)
+    for part in rest[: HALVES * HALVES]:
         part[...] = jnp.zeros_like(part)
 
     def step(i, carry):
         fill_basis(basis, ytab, ztab, i)
         held = step_blocks(i, steps, blocks)
-        start_next(i, steps, blocks, [load])
-        for b in held:
-            load(b).wait()
-        for x0 in range(0, xl, xn):
-            values = [grid_rows(fbuf.at[b], x0, xn, yb) for b in held]
-            forward_sums(values, basis, acc, x0, xn)
+        start_next(i, steps, blocks, loads)
+        for h in range(HALVES):
+            for b in held:
+                loads[h](b).wait()
+            for x0 in range(0, xl, xn):
+                values = [grid_rows(fbuf.at[h, b], x0, xn, yb) for b in held]
+                forward_sums(values, basis, acc[h], x0, xn)
         return carry
 
     lax.fori_loop(0, steps, step, 0)
-    x_forward_store(acc, xf[0], out, xf.shape[1] // SUB)
+    for h in range(HALVES):
+        x_forward_store(acc[h], xf[0], out.at[:, :, h], xf.shape[1] // SUB)
 
 
 def slope_kernel(rank, spec, mix, ytab, ztab, xf, xi, field, cot, *rest, xn, jo, first):
@@ -387,10 +390,14 @@
     lax.fori_loop(0, outer, body, 0)
 
 
-def apply_kernel(got_a, got_b, weights, out_a, out_b, masked, ua, ub, va, vb, *, pencil, size, folded):
+def apply_kernel(
+    got, weights, out_a, out_b, masked, ua, ub, va, vb, *, pencil, size, folded
+):
     outer, halves, kh, ch, wide = weights.shape
-    samples = got_a.shape[0] // pencil
-    total = got_a.shape[1]
+    samples = got.shape[0] // pencil
+    total = outer * kh
+    got_a = got.at[:, pl.ds(0, total)]
+    got_b = got.at[:, pl.ds(total, total)]
     gather_partials(got_a, ua, pencil, 1.0)
     gather_partials(got_b, ub, pencil, 1.0)
 
@@ -600,27 +607,31 @@
         store = pltpu.VMEM((samples * owned, wide), F32)
         options = dict(pencil=pencil, size=size, folded=folded)
 
-        yb = 8
-        got = []
-        for h in range(HALVES):
-            modes_h = call(
-                functools.partial(forward_kernel, xn=xn, jo=jo, first=h * hc),
-                yb,
-                [anywhere, y_spec(yb), z_spec, ranked(xf)],
-                whole(packed),
-                spectrum,
-                [*basis(yb), *acc, held(yb, hc), sems(1, yb)],
-                "field_modes_%d" % h,
-                (sample, y_table(yb), ztab, xf),
-                work,
-            )
-            if got:
-                modes_h, got[0] = lax.optimization_barrier((modes_h, got[0]))
-            got.append(exchange(modes_h))
+        yb = FIELD_ROWS
+        both = packed[:2] + (HALVES,) + packed[2:]
+        sent = call(
+            functools.partial(forward_kernel, xn=xn, jo=jo),
+            yb,
+            [anywhere, y_spec(yb), z_spec, ranked(xf)],
+            whole(both),
+            jax.ShapeDtypeStruct(both, BF16),
+            [
+                *basis(yb),
+                *acc,
+                *acc,
+                pltpu.VMEM((HALVES, ny // yb, xl, yb, hc, nz), BF16),
+                sems(HALVES, yb),
+            ],
+            "field_modes",
+            (sample, y_table(yb), ztab, xf),
+            2 * work,
+        )
+        paired = (dp * pencil, HALVES * owned, wide)
+        got = lax.all_to_all(sent.reshape(paired), ("dp", "pencil"), 0, 0, tiled=True)
         va, vb, masked = owner_call(
             functools.partial(apply_kernel, **options),
-            (got[0], got[1], weights),
-            [whole(flat), whole(flat), whole(weights.shape)],
+            (got, weights),
+            [whole(paired), whole(weights.shape)],
             (whole(flat), whole(flat), whole(line_shape.shape)),
             (message, message, line_shape),
             [store] * 4,

time: 202 us -> 199 us (0.985)
  blocking collectives: 39.8 us -> 54.8 us
  waiting for transfers between devices: 33.2 us -> 25.7 us
  starting transfers between devices: 25.6 us -> 18.4 us
  Pallas kernels: 97.1 us -> 94.2 us
    all_to_all x0 -> x1, blocking collectives: none -> 33.5 us  [body(): lax.all_to_all(sent.reshape(paired), ('dp', 'pencil'), 0, 0, tiled=True)]
    all_to_all x2 -> x1, blocking collectives: 39.8 us -> 21.2 us  [exchange(): lax.all_to_all(values.reshape(flat), ('dp', 'pencil'), 0, 0, tiled=True)]
    all_to_all x6 -> x5, waiting for transfers between devices: 33.2 us -> 25.7 us  [exchange(): lax.all_to_all(values.reshape(flat), ('dp', 'pencil'), 0, 0, tiled=True)]
    all_to_all x6 -> x5, starting transfers between devices: 25.6 us -> 18.4 us  [exchange(): lax.all_to_all(values.reshape(flat), ('dp', 'pencil'), 0, 0, tiled=True)]
    pallas_call x6 -> x5, Pallas kernels: 81.2 us -> 78.3 us  [call(): pl.pallas_call(kernel, grid_spec=pltpu.PrefetchScalarGridSpec(num_scalar_...]
  transfers between devices with their start and end apart: 6 -> 5, of which waited for: 4 -> 3; matrix products, arithmetic and copies ran while one was open for 2% -> 2% of each run, Pallas kernels for 33% -> 29%
where the time goes in v3:
time: 199 us
  Pallas kernels  94.2 us (47%)
  blocking collectives  54.8 us (28%)
  waiting for transfers between devices  25.7 us (13%)
  starting transfers between devices  18.4 us (9%)
  local copies, waits for them, and re-layouts  4.16 us (2%)
    pallas_call x5, Pallas kernels, call(): pl.pallas_call(kernel, grid_spec=pltpu.PrefetchScalarGridSpec(num_scalar_...  78.3 us
    all_to_all x1, blocking collectives, body(): lax.all_to_all(sent.reshape(paired), ('dp', 'pencil'), 0, 0, tiled=True)  33.5 us
    all_to_all x5, waiting for transfers between devices, exchange(): lax.all_to_all(values.reshape(flat), ('dp', 'pencil'), 0, 0, tiled=True)  25.7 us
    all_to_all x1, blocking collectives, exchange(): lax.all_to_all(values.reshape(flat), ('dp', 'pencil'), 0, 0, tiled=True)  21.2 us
    all_to_all x5, starting transfers between devices, exchange(): lax.all_to_all(values.reshape(flat), ('dp', 'pencil'), 0, 0, tiled=True)  18.4 us
    pallas_call x3, Pallas kernels, owner_call(): pl.pallas_call(kernel, grid=(steps,), in_specs=ins, out_specs=outs, out_s...  15.9 us
  transfers between devices with their start and end apart: 5, of which 3 were waited for; matrix products, arithmetic and copies ran while one was open for 2% of the time, Pallas kernels for 29%

profile of v3, /device:TPU:1, one launch (start us, length us, event | category | flops | bytes accessed | tf_op | source)
XLA Modules:
  0.0 198.5 jit_solution(5795543971257607619)
XLA Ops:
  0.6 12.7 %field_modes.1 = bf16[8,4,2,2,32,128]{5,4,3,2,1,0:T(8,128)(2,1)} custom-call(s32[1]{0:T(128)} %bitcast.rank, bf16[16,64,64,128]{3,2,1,0:T(8,128)(2,1)} %bitcast.14, f32[2,2,8,4,128]{4,3,2,1,0:T(4,128)} %constant.14.clone.ytab, f32[2,2,128,128]{3,2,1,0:T(8,128)} %constant.15.clone.ztab, bf16[4,256,512]{2,1,0:T(8,128)(2,1)} %constant.16.clone.xf), custom_call_target="tpu_custom_call" | custom-call | flops 8589934592 | bytes 16777216 | tf_op jit(solution)/shard_map/field_modes/pallas_call | solution.py:556
  13.4 33.5 %all_to_all.35.got = bf16[32,128,128]{2,1,0:T(8,128)(2,1)} all-to-all(bf16[32,128,128]{2,1,0:T(8,128)(2,1)} %bitcast.20), channel_id=1, replica_groups=mesh['dp'=8,'pencil'=4] {'dp','pencil'}, dimensions={0} | all-to-all | bytes 2097152 | tf_op jit(solution)/shard_map/all_to_all | solution.py:630
  46.9 5.5 %apply_modes.1 = (bf16[32,64,128]{2,1,0:T(8,128)(2,1)}, bf16[32,64,128]{2,1,0:T(8,128)(2,1)}, bf16[64,32,128]{2,1,0:T(8,128)(2,1)}) custom-call(bf16[32,128,128]{2,1,0:T(8,128)(2,1)} %all_to_all.35.got, bf16[4,2,16,64,128]{4,3,2,1,0:T(8,128)(2,1)} %bitcast.23), custom_call_target="tpu_custom_call" | custom-call | flops 1073741824 | bytes 2097152 | tf_op jit(solution)/shard_map/apply_modes/pallas_call | solution.py:588
  52.4 3.2 %all-to-all-start.2 = ((bf16[32,64,128]{2,1,0:T(8,128)(2,1)}), bf16[32,64,128]{2,1,0:T(8,128)(2,1)S(1)}, u32[]{:S(2)}, u32[]{:S(2)}) async-start(bf16[32,64,128]{2,1,0:T(8,128)(2,1)} %get-tuple-element.20), calls=%async_computation.2 | async-start | bytes 1048576 | tf_op jit(solution)/shard_map/all_to_all | solution.py:585
  55.9 0.3 broadcast_multiply_fusion
  56.1 0.8 mul.87.mix
  56.9 0.8 mul.84.mix
  57.7 13.2 %all-to-all-done.2.spec = bf16[32,64,128]{2,1,0:T(8,128)(2,1)S(1)} async-done(((bf16[32,64,128]{2,1,0:T(8,128)(2,1)}), bf16[32,64,128]{2,1,0:T(8,128)(2,1)S(1)}, u32[]{:S(2)}, u32[]{:S(2)}) %all-to-all-start.2) | async-done | bytes 524320 | tf_op jit(solution)/shard_map/all_to_all | solution.py:585
  70.8 3.2 %all-to-all-start.1 = ((bf16[32,64,128]{2,1,0:T(8,128)(2,1)}), bf16[32,64,128]{2,1,0:T(8,128)(2,1)S(1)}, u32[]{:S(2)}, u32[]{:S(2)}) async-start(bf16[32,64,128]{2,1,0:T(8,128)(2,1)} %get-tuple-element.19), calls=%async_computation.1 | async-start | bytes 1048576 | tf_op jit(solution)/shard_map/all_to_all | solution.py:585
  74.0 21.0 %slope_modes_0.1 = (bf16[16,64,64,128]{3,2,1,0:T(8,128)(2,1)}, bf16[8,4,2,32,128]{4,3,2,1,0:T(8,128)(2,1)}) custom-call(s32[1]{0:T(128)} %bitcast.rank, bf16[32,64,128]{2,1,0:T(8,128)(2,1)} %copy-done.3, bf16[128,256]{1,0:T(8,128)(2,1)} %mul.87.mix, f32[2,2,8,4,128]{4,3,2,1,0:T(4,128)} %constant.14.clone.ytab, f32[2,2,128,128]{3,2,1,0:T(8,128)} %constant.15.clone.ztab, ...), custom_call_target="tpu_custom_call" | custom-call | flops 12884901888 | bytes 16777216 | tf_op jit(solution)/shard_map/slope_modes_0/pallas_call | solution.py:556
  95.0 5.8 %all-to-all-start.3 = ((bf16[32,64,128]{2,1,0:T(8,128)(2,1)}), bf16[32,64,128]{2,1,0:T(8,128)(2,1)S(1)}, u32[]{:S(2)}, u32[]{:S(2)}) async-start(bf16[32,64,128]{2,1,0:T(8,128)(2,1)} %bitcast.21), calls=%async_computation.3 | async-start | bytes 1048576 | tf_op jit(solution)/shard_map/all_to_all | solution.py:585
  100.9 21.0 %slope_modes_1.1 = (bf16[16,64,64,128]{3,2,1,0:T(8,128)(2,1)}, bf16[8,4,2,32,128]{4,3,2,1,0:T(8,128)(2,1)}) custom-call(s32[1]{0:T(128)} %bitcast.rank, bf16[32,64,128]{2,1,0:T(8,128)(2,1)} %copy-done.1, bf16[128,256]{1,0:T(8,128)(2,1)} %mul.84.mix, f32[2,2,8,4,128]{4,3,2,1,0:T(4,128)} %constant.14.clone.ytab, ...), custom_call_target="tpu_custom_call", output_to_operand_aliasing={{0}: (9, {})} | custom-call | flops 12884901888 | bytes 16777216 | tf_op jit(solution)/shard_map/slope_modes_1/pallas_call | solution.py:556
  121.9 21.2 %all_to_all.36.got_b = bf16[32,64,128]{2,1,0:T(8,128)(2,1)} all-to-all(bf16[32,64,128]{2,1,0:T(8,128)(2,1)} %bitcast.22), channel_id=1, replica_groups=mesh['dp'=8,'pencil'=4] {'dp','pencil'}, dimensions={0} | all-to-all | bytes 1048576 | tf_op jit(solution)/shard_map/all_to_all | solution.py:585
  143.1 5.8 %adjoint_modes.1 = (bf16[32,64,128]{2,1,0:T(8,128)(2,1)}, bf16[32,64,128]{2,1,0:T(8,128)(2,1)}, bf16[64,32,128]{2,1,0:T(8,128)(2,1)}) custom-call(bf16[32,64,128]{2,1,0:T(8,128)(2,1)} %copy-done.4, bf16[32,64,128]{2,1,0:T(8,128)(2,1)} %all_to_all.36.got_b, bf16[4,2,16,64,128]{4,3,2,1,0:T(8,128)(2,1)} %bitcast.24), custom_call_target="tpu_custom_call" | custom-call | flops 1073741824 | bytes 2097152 | tf_op jit(solution)/shard_map/adjoint_modes/pallas_call | solution.py:588
  148.9 3.2 %all-to-all-start.5 = ((bf16[32,64,128]{2,1,0:T(8,128)(2,1)}), bf16[32,64,128]{2,1,0:T(8,128)(2,1)S(1)}, u32[]{:S(2)}, u32[]{:S(2)}) async-start(bf16[32,64,128]{2,1,0:T(8,128)(2,1)} %get-tuple-element.27), calls=%async_computation.5 | async-start | bytes 1048576 | tf_op jit(solution)/shard_map/all_to_all | solution.py:585
  152.0 0.8 mul.95.mix
  152.8 0.8 mul.92.mix
  153.6 4.6 %weight_grads.1 = f32[4,2,16,64,128]{4,3,2,1,0:T(8,128)} custom-call(bf16[64,32,128]{2,1,0:T(8,128)(2,1)} %get-tuple-element.28.masked, bf16[64,32,128]{2,1,0:T(8,128)(2,1)} %get-tuple-element.29.stacked), custom_call_target="tpu_custom_call" | custom-call | flops 1073741824 | bytes 2097152 | tf_op jit(solution)/shard_map/weight_grads/pallas_call | solution.py:588
  158.2 9.1 %all-to-all-done.5.spec = bf16[32,64,128]{2,1,0:T(8,128)(2,1)S(1)} async-done(((bf16[32,64,128]{2,1,0:T(8,128)(2,1)}), bf16[32,64,128]{2,1,0:T(8,128)(2,1)S(1)}, u32[]{:S(2)}, u32[]{:S(2)}) %all-to-all-start.5) | async-done | bytes 524320 | tf_op jit(solution)/shard_map/all_to_all | solution.py:585
  167.3 3.2 %all-to-all-start.6 = ((bf16[32,64,128]{2,1,0:T(8,128)(2,1)}), bf16[32,64,128]{2,1,0:T(8,128)(2,1)S(1)}, u32[]{:S(2)}, u32[]{:S(2)}) async-start(bf16[32,64,128]{2,1,0:T(8,128)(2,1)} %get-tuple-element.30), calls=%async_computation.6 | async-start | bytes 1048576 | tf_op jit(solution)/shard_map/all_to_all | solution.py:585
  170.5 11.8 %grad_field_0.1.rest_0_ = bf16[16,64,64,128]{3,2,1,0:T(8,128)(2,1)} custom-call(s32[1]{0:T(128)} %bitcast.rank, bf16[32,64,128]{2,1,0:T(8,128)(2,1)} %copy-done, bf16[128,256]{1,0:T(8,128)(2,1)} %mul.92.mix, f32[2,2,8,4,128]{4,3,2,1,0:T(4,128)} %constant.14.clone.ytab, f32[2,2,128,128]{3,2,1,0:T(8,128)} %constant.15.clone.ztab, ...), custom_call_target="tpu_custom_call" | custom-call | flops 8589934592 | bytes 16777216 | tf_op jit(solution)/shard_map/grad_field_0/pallas_call | solution.py:556
  182.3 3.4 %all-to-all-done.6.spec = bf16[32,64,128]{2,1,0:T(8,128)(2,1)S(1)} async-done(((bf16[32,64,128]{2,1,0:T(8,128)(2,1)}), bf16[32,64,128]{2,1,0:T(8,128)(2,1)S(1)}, u32[]{:S(2)}, u32[]{:S(2)}) %all-to-all-start.6) | async-done | bytes 524320 | tf_op jit(solution)/shard_map/all_to_all | solution.py:585
  185.7 0.8 copy-done.2
  186.5 11.8 %grad_field_1.1 = bf16[16,64,64,128]{3,2,1,0:T(8,128)(2,1)} custom-call(s32[1]{0:T(128)} %bitcast.rank, bf16[32,64,128]{2,1,0:T(8,128)(2,1)} %copy-done.2, bf16[128,256]{1,0:T(8,128)(2,1)} %mul.95.mix, f32[2,2,8,4,128]{4,3,2,1,0:T(4,128)} %constant.14.clone.ytab, f32[2,2,128,128]{3,2,1,0:T(8,128)} %constant.15.clone.ztab, ...), custom_call_target="tpu_custom_call", output_to_operand_aliasing={{}: (7, {})} | custom-call | flops 8589934592 | bytes 16777216 | tf_op jit(solution)/shard_map/grad_field_1/pallas_call | solution.py:556
  (19 shorter events, 0.3 us)
Async XLA Ops:
  0.6 54.9 %copy-start.5 = (bf16[64,64]{1,0:T(8,128)(2,1)S(1)}, bf16[64,64]{1,0:T(8,128)(2,1)}, u32[]{:S(2)}) copy-start(bf16[64,64]{1,0:T(8,128)(2,1)} %param.15) | copy-start | bytes 24580
  52.4 18.4 %all-to-all-start.2 = ((bf16[32,64,128]{2,1,0:T(8,128)(2,1)}), bf16[32,64,128]{2,1,0:T(8,128)(2,1)S(1)}, u32[]{:S(2)}, u32[]{:S(2)}) async-start(bf16[32,64,128]{2,1,0:T(8,128)(2,1)} %get-tuple-element.20), calls=%async_computation.2 | async-start | bytes 1048576 | tf_op jit(solution)/shard_map/all_to_all | solution.py:585
  70.8 3.2 %copy-start.3 = (bf16[32,64,128]{2,1,0:T(8,128)(2,1)}, bf16[32,64,128]{2,1,0:T(8,128)(2,1)S(1)}, u32[]{:S(2)}) copy-start(bf16[32,64,128]{2,1,0:T(8,128)(2,1)S(1)} %all-to-all-done.2.spec) | copy-start | bytes 1572868
  70.8 24.2 %all-to-all-start.1 = ((bf16[32,64,128]{2,1,0:T(8,128)(2,1)}), bf16[32,64,128]{2,1,0:T(8,128)(2,1)S(1)}, u32[]{:S(2)}, u32[]{:S(2)}) async-start(bf16[32,64,128]{2,1,0:T(8,128)(2,1)} %get-tuple-element.19), calls=%async_computation.1 | async-start | bytes 1048576 | tf_op jit(solution)/shard_map/all_to_all | solution.py:585
  95.0 5.9 %copy-start.1 = (bf16[32,64,128]{2,1,0:T(8,128)(2,1)}, bf16[32,64,128]{2,1,0:T(8,128)(2,1)S(1)}, u32[]{:S(2)}) copy-start(bf16[32,64,128]{2,1,0:T(8,128)(2,1)S(1)} %all-to-all-done.1.spec) | copy-start | bytes 1572868
  95.0 26.8 %all-to-all-start.3 = ((bf16[32,64,128]{2,1,0:T(8,128)(2,1)}), bf16[32,64,128]{2,1,0:T(8,128)(2,1)S(1)}, u32[]{:S(2)}, u32[]{:S(2)}) async-start(bf16[32,64,128]{2,1,0:T(8,128)(2,1)} %bitcast.21), calls=%async_computation.3 | async-start | bytes 1048576 | tf_op jit(solution)/shard_map/all_to_all | solution.py:585
  121.9 21.2 %copy-start.4 = (bf16[32,64,128]{2,1,0:T(8,128)(2,1)}, bf16[32,64,128]{2,1,0:T(8,128)(2,1)S(1)}, u32[]{:S(2)}) copy-start(bf16[32,64,128]{2,1,0:T(8,128)(2,1)S(1)} %all-to-all-done.3.got_a) | copy-start | bytes 1572868
  148.9 18.4 %all-to-all-start.5 = ((bf16[32,64,128]{2,1,0:T(8,128)(2,1)}), bf16[32,64,128]{2,1,0:T(8,128)(2,1)S(1)}, u32[]{:S(2)}, u32[]{:S(2)}) async-start(bf16[32,64,128]{2,1,0:T(8,128)(2,1)} %get-tuple-element.27), calls=%async_computation.5 | async-start | bytes 1048576 | tf_op jit(solution)/shard_map/all_to_all | solution.py:585
  167.3 3.2 %copy-start = (bf16[32,64,128]{2,1,0:T(8,128)(2,1)}, bf16[32,64,128]{2,1,0:T(8,128)(2,1)S(1)}, u32[]{:S(2)}) copy-start(bf16[32,64,128]{2,1,0:T(8,128)(2,1)S(1)} %all-to-all-done.5.spec) | copy-start | bytes 1572868
  167.3 18.4 %all-to-all-start.6 = ((bf16[32,64,128]{2,1,0:T(8,128)(2,1)}), bf16[32,64,128]{2,1,0:T(8,128)(2,1)S(1)}, u32[]{:S(2)}, u32[]{:S(2)}) async-start(bf16[32,64,128]{2,1,0:T(8,128)(2,1)} %get-tuple-element.30), calls=%async_computation.6 | async-start | bytes 1048576 | tf_op jit(solution)/shard_map/all_to_all | solution.py:585
  185.7 0.8 copy-start.2
